TPU v7x, 8 devices: a whole 2x2x1 slice. The times are simulated.
8 devices in a mesh: dp: 1 (over z), tp: 8 (over y, x, core).
Axes of the slice: x: 2, y: 2, z: 1, core: 2. Of those that a mesh axis runs over, the one named last changes fastest.
Arguments:
- x_in: bfloat16 [1, 2048, 1536], P('dp', 'tp')
- y_grad: bfloat16 [1, 2048, 1536], P('dp', 'tp')
- ln_par: float32 [2, 4, 1536], replicated
- bias_d: float32 [2, 2, 1536], replicated
- w_qkv: bfloat16 [2, 1536, 3, 16, 96], P(None, None, None, 'tp')
- w_out: bfloat16 [2, 16, 96, 1536], P(None, 'tp')
- w_up: bfloat16 [2, 1536, 6144], P(None, None, 'tp')
- b_up: float32 [2, 6144], P(None, 'tp')
- w_down: bfloat16 [2, 6144, 1536], P(None, 'tp')
Outputs:
- output 1: bfloat16 [1, 2048, 1536], P('dp', 'tp')
- output 2: bfloat16 [1, 2048, 1536], P('dp', 'tp')
- output 3: float32 [2, 4, 1536], P('dp')
- output 4: float32 [2, 2, 1536], P('dp')
- output 5: bfloat16 [2, 1536, 3, 16, 96], P('dp', None, None, 'tp')
- output 6: bfloat16 [2, 16, 96, 1536], P('dp', 'tp')
- output 7: bfloat16 [2, 1536, 6144], P('dp', None, 'tp')
- output 8: float32 [2, 6144], P('dp', 'tp')
- output 9: bfloat16 [2, 6144, 1536], P('dp', 'tp')
All inputs are finite; a program needn't handle non-finite values.
Results may differ from a plain program's by a relative error of at most 0.02.
Values are sent between devices in bfloat16 or wider.
A program may use at most 1 GiB of HBM per device.

v0:
```python
import jax
import jax.numpy as jnp
from jax import lax
from jax.sharding import PartitionSpec as P


def layer_norm(row_vals, ln_gain, ln_shift):
    mean_val = jnp.mean(row_vals, axis=-1, keepdims=True)
    centered = row_vals - mean_val
    var_val = jnp.mean(centered * centered, axis=-1, keepdims=True)
    return centered * lax.rsqrt(var_val + 1e-5) * ln_gain + ln_shift


def gelu_tanh(pre_act):
    return jax.nn.gelu(pre_act, approximate=True)


def gather_rows(local_vals):
    return lax.all_gather(local_vals, 'tp', axis=1, tiled=True)


def scatter_rows(partial_vals, group_size):
    n_batch, seq_len, width = partial_vals.shape
    sent = partial_vals.astype(jnp.bfloat16).reshape(n_batch, group_size, seq_len // group_size, width)
    received = lax.all_to_all(sent, 'tp', 1, 1, tiled=True)
    return jnp.sum(received, axis=1, dtype=jnp.float32)


def causal_attention(q_vals, k_vals, v_vals):
    seq_len = q_vals.shape[1]
    score_scale = q_vals.shape[-1] ** -0.5
    scores = jnp.einsum('bqhe,bkhe->bhqk', q_vals, k_vals, preferred_element_type=jnp.float32) * score_scale
    positions = jnp.arange(seq_len)
    causal = positions[:, None] >= positions[None, :]
    scores = jnp.where(causal, scores, -1e30)
    prob_bf = jax.nn.softmax(scores, axis=-1).astype(jnp.bfloat16)
    attn_vals = jnp.einsum('bhqk,bkhe->bqhe', prob_bf, v_vals, preferred_element_type=jnp.float32).astype(jnp.bfloat16)
    return attn_vals, prob_bf


def attention_backward(d_attn, q_vals, k_vals, v_vals, prob_bf):
    score_scale = q_vals.shape[-1] ** -0.5
    d_prob = jnp.einsum('bqhe,bkhe->bhqk', d_attn, v_vals, preferred_element_type=jnp.float32)
    d_v = jnp.einsum('bhqk,bqhe->bkhe', prob_bf, d_attn, preferred_element_type=jnp.float32)
    row_dot = jnp.sum(d_prob * prob_bf, axis=-1, keepdims=True)
    d_score = (prob_bf * (d_prob - row_dot) * score_scale).astype(jnp.bfloat16)
    d_q = jnp.einsum('bhqk,bkhe->bqhe', d_score, k_vals, preferred_element_type=jnp.float32)
    d_k = jnp.einsum('bhqk,bqhe->bkhe', d_score, q_vals, preferred_element_type=jnp.float32)
    return d_q, d_k, d_v


def solution(mesh):
    group_size = mesh.shape['tp']

    def device_step(x_loc, dy_loc, ln_par, bias_d, w_qkv, w_out, w_up, b_up, w_down):
        n_layers = ln_par.shape[0]
        residual = x_loc.astype(jnp.float32)
        saved = []
        for layer_idx in range(n_layers):
            ln_vals = ln_par[layer_idx]
            bias_vals = bias_d[layer_idx]
            w_proj = w_qkv[layer_idx]
            res_one = residual
            h_all = gather_rows(layer_norm(res_one, ln_vals[0], ln_vals[1]).astype(jnp.bfloat16))
            q_vals = jnp.einsum('bsd,dhe->bshe', h_all, w_proj[:, 0], preferred_element_type=jnp.float32).astype(jnp.bfloat16)
            k_vals = jnp.einsum('bsd,dhe->bshe', h_all, w_proj[:, 1], preferred_element_type=jnp.float32).astype(jnp.bfloat16)
            v_vals = jnp.einsum('bsd,dhe->bshe', h_all, w_proj[:, 2], preferred_element_type=jnp.float32).astype(jnp.bfloat16)
            attn_vals, prob_bf = causal_attention(q_vals, k_vals, v_vals)
            attn_part = jnp.einsum('bshe,hed->bsd', attn_vals, w_out[layer_idx], preferred_element_type=jnp.float32)
            res_two = res_one + scatter_rows(attn_part, group_size) + bias_vals[0]
            h2_all = gather_rows(layer_norm(res_two, ln_vals[2], ln_vals[3]).astype(jnp.bfloat16))
            pre_act = jnp.einsum('bsd,df->bsf', h2_all, w_up[layer_idx], preferred_element_type=jnp.float32) + b_up[layer_idx]
            act_f, gelu_pull = jax.vjp(gelu_tanh, pre_act)
            act_vals = act_f.astype(jnp.bfloat16)
            mlp_part = jnp.einsum('bsf,fd->bsd', act_vals, w_down[layer_idx], preferred_element_type=jnp.float32)
            residual = res_two + scatter_rows(mlp_part, group_size) + bias_vals[1]
            saved.append((res_one, h_all, q_vals, k_vals, v_vals, prob_bf, attn_vals, res_two, h2_all, gelu_pull, act_vals))
        y_loc = residual.astype(jnp.bfloat16)

        d_res = dy_loc.astype(jnp.float32)
        layer_grads = [None] * n_layers
        for layer_idx in reversed(range(n_layers)):
            res_one, h_all, q_vals, k_vals, v_vals, prob_bf, attn_vals, res_two, h2_all, gelu_pull, act_vals = saved[layer_idx]
            ln_vals = ln_par[layer_idx]
            w_proj = w_qkv[layer_idx]
            d_bias_two = jnp.sum(d_res, axis=(0, 1))
            d_mlp_all = gather_rows(d_res.astype(jnp.bfloat16))
            d_wdown = jnp.einsum('bsf,bsd->fd', act_vals, d_mlp_all, preferred_element_type=jnp.float32)
            d_act = jnp.einsum('bsd,fd->bsf', d_mlp_all, w_down[layer_idx], preferred_element_type=jnp.float32)
            d_pre = gelu_pull(d_act)[0]
            d_bup = jnp.sum(d_pre, axis=(0, 1))
            d_pre_bf = d_pre.astype(jnp.bfloat16)
            d_wup = jnp.einsum('bsd,bsf->df', h2_all, d_pre_bf, preferred_element_type=jnp.float32)
            d_h2 = scatter_rows(jnp.einsum('bsf,df->bsd', d_pre_bf, w_up[layer_idx], preferred_element_type=jnp.float32), group_size)
            ln_pull = jax.vjp(layer_norm, res_two, ln_vals[2], ln_vals[3])[1]
            d_mid, d_gain_two, d_shift_two = ln_pull(d_h2)
            d_res = d_res + d_mid
            d_bias_one = jnp.sum(d_res, axis=(0, 1))
            d_attn_all = gather_rows(d_res.astype(jnp.bfloat16))
            d_wout = jnp.einsum('bshe,bsd->hed', attn_vals, d_attn_all, preferred_element_type=jnp.float32)
            d_attn = jnp.einsum('bsd,hed->bshe', d_attn_all, w_out[layer_idx], preferred_element_type=jnp.float32).astype(jnp.bfloat16)
            d_q, d_k, d_v = attention_backward(d_attn, q_vals, k_vals, v_vals, prob_bf)
            d_proj = [d_q.astype(jnp.bfloat16), d_k.astype(jnp.bfloat16), d_v.astype(jnp.bfloat16)]
            d_wqkv = jnp.stack([jnp.einsum('bsd,bshe->dhe', h_all, d_part, preferred_element_type=jnp.float32) for d_part in d_proj], axis=1)
            d_h_part = (jnp.einsum('bshe,dhe->bsd', d_proj[0], w_proj[:, 0], preferred_element_type=jnp.float32)
                        + jnp.einsum('bshe,dhe->bsd', d_proj[1], w_proj[:, 1], preferred_element_type=jnp.float32)
                        + jnp.einsum('bshe,dhe->bsd', d_proj[2], w_proj[:, 2], preferred_element_type=jnp.float32))
            d_h = scatter_rows(d_h_part, group_size)
            ln_pull = jax.vjp(layer_norm, res_one, ln_vals[0], ln_vals[1])[1]
            d_in, d_gain_one, d_shift_one = ln_pull(d_h)
            d_res = d_res + d_in
            layer_grads[layer_idx] = (jnp.stack([d_gain_one, d_shift_one, d_gain_two, d_shift_two]), jnp.stack([d_bias_one, d_bias_two]), d_wqkv, d_wout, d_wup, d_bup, d_wdown)
        small_grads = lax.psum((jnp.stack([grad_set[0] for grad_set in layer_grads]), jnp.stack([grad_set[1] for grad_set in layer_grads])), 'tp')
        return (y_loc, d_res.astype(jnp.bfloat16), small_grads[0], small_grads[1],
                jnp.stack([grad_set[2] for grad_set in layer_grads]).astype(jnp.bfloat16),
                jnp.stack([grad_set[3] for grad_set in layer_grads]).astype(jnp.bfloat16),
                jnp.stack([grad_set[4] for grad_set in layer_grads]).astype(jnp.bfloat16),
                jnp.stack([grad_set[5] for grad_set in layer_grads]),
                jnp.stack([grad_set[6] for grad_set in layer_grads]).astype(jnp.bfloat16))

    in_specs = (P('dp', 'tp', None), P('dp', 'tp', None), P(None, None, None), P(None, None, None),
                P(None, None, None, 'tp', None), P(None, 'tp', None, None), P(None, None, 'tp'), P(None, 'tp'), P(None, 'tp', None))
    out_specs = (P('dp', 'tp', None), P('dp', 'tp', None), P('dp', None, None), P('dp', None, None),
                 P('dp', None, None, 'tp', None), P('dp', 'tp', None, None), P('dp', None, 'tp'), P('dp', 'tp'), P('dp', 'tp', None))
    return jax.shard_map(device_step, mesh=mesh, in_specs=in_specs, out_specs=out_specs, check_vma=False)
```

profile of v0, /device:TPU:0, one launch (start us, length us, event | category | flops | bytes accessed | tf_op | source)
XLA Modules:
  0.0 1441.4 jit_solution(17611317616704184383)
XLA Ops:
  23.1 34.9 %all-gather.9.cloned.1.call-done = bf16[1,2048,1536]{2,1,0:T(8,128)(2,1)} async-done(((bf16[1,256,1536]{2,1,0:T(8,128)(2,1)}), bf16[1,2048,1536]{2,1,0:T(8,128)(2,1)}) %all-gather.9.cloned.1.call-update) | async-done | bytes 6291472 | tf_op jit(solution)/shard_map/all_gather | solution.py:19
  66.5 19.5 %fusion.267 = (f32[2,2048]{1,0:T(2,128)S(1)}, f32[2,2048,2048]{1,2,0:T(8,128)}) fusion(pred[2048,2048]{0,1:T(8,128)(4,1)} %iota_compare_fusion, f32[2048,2,96]{0,2,1:T(8,128)} %bitcast.454, f32[2048,2,96]{0,2,1:T(8,128)S(1)} %bitcast.452), kind=kOutput, calls=%fused_computation.347 | convolution fusion | flops 1644955648 | bytes 40910848 | tf_op jit(solution)/shard_map/sub | solution.py:36
  86.0 12.7 divide_convert_fusion.1
  98.7 9.5 fusion.82
  119.8 70.8 %all-to-all-done = bf16[1,8,256,1536]{3,2,0,1:T(8,128)(2,1)} async-done(((bf16[1,8,256,1536]{3,2,0,1:T(8,128)(2,1)}), bf16[1,8,256,1536]{3,2,0,1:T(8,128)(2,1)}, u32[]{:S(2)}, u32[]{:S(2)}) %all-to-all-start) | async-done | bytes 6291488 | tf_op jit(solution)/shard_map/all_to_all | solution.py:25
  196.5 38.7 %all-gather.11.cloned.1.call-done = bf16[1,2048,1536]{2,1,0:T(8,128)(2,1)} async-done(((bf16[1,256,1536]{2,1,0:T(8,128)(2,1)}), bf16[1,2048,1536]{2,1,0:T(8,128)(2,1)}) %all-gather.11.cloned.1.call-update) | async-done | bytes 6291472 | tf_op jit(solution)/shard_map/all_gather | solution.py:19
  235.2 8.0 fusion.70
  243.3 9.3 convolution_convert_fusion.3
  252.7 72.8 %all_to_all.40 = bf16[1,8,256,1536]{3,2,0,1:T(8,128)(2,1)S(1)} all-to-all(bf16[1,8,256,1536]{3,2,0,1:T(8,128)(2,1)S(1)} %bitcast.424), channel_id=1, replica_groups=mesh['dp'=1,'tp'=8] {'tp'}, dimensions={1} | all-to-all | bytes 12582912 | tf_op jit(solution)/shard_map/all_to_all | solution.py:25
  328.4 38.7 %all-gather.13.cloned.1.call-done = bf16[1,2048,1536]{2,1,0:T(8,128)(2,1)} async-done(((bf16[1,256,1536]{2,1,0:T(8,128)(2,1)}), bf16[1,2048,1536]{2,1,0:T(8,128)(2,1)}) %all-gather.13.cloned.1.call-update) | async-done | bytes 6291472 | tf_op jit(solution)/shard_map/all_gather | solution.py:19
  376.8 20.3 %fusion.276 = (f32[2,2048]{1,0:T(2,128)S(1)}, f32[2,2048,2048]{1,2,0:T(8,128)}) fusion(pred[2048,2048]{0,1:T(8,128)(4,1)} %iota_compare_fusion, f32[2048,2,96]{0,2,1:T(8,128)} %bitcast.458, f32[2048,2,96]{0,2,1:T(8,128)} %bitcast.456), kind=kOutput, calls=%fused_computation.348 | convolution fusion | flops 1644955648 | bytes 40910848 | tf_op jit(solution)/shard_map/sub | solution.py:36
  397.1 12.7 divide_convert_fusion
  409.8 9.5 fusion.66
  424.1 72.8 %all_to_all.41 = bf16[1,8,256,1536]{3,2,0,1:T(8,128)(2,1)S(1)} all-to-all(bf16[1,8,256,1536]{3,2,0,1:T(8,128)(2,1)S(1)} %bitcast.413), channel_id=1, replica_groups=mesh['dp'=1,'tp'=8] {'tp'}, dimensions={1} | all-to-all | bytes 12582912 | tf_op jit(solution)/shard_map/all_to_all | solution.py:25
  500.4 38.2 %all-gather.15.cloned.1.call-done = bf16[1,2048,1536]{2,1,0:T(8,128)(2,1)} async-done(((bf16[1,256,1536]{2,1,0:T(8,128)(2,1)}), bf16[1,2048,1536]{2,1,0:T(8,128)(2,1)}) %all-gather.15.cloned.1.call-update) | async-done | bytes 6291472 | tf_op jit(solution)/shard_map/all_gather | solution.py:19
  538.6 9.6 fusion.54
  548.2 31.6 %all-gather.17.cloned.1.call-done = bf16[1,2048,1536]{2,1,0:T(8,128)(2,1)} async-done(((bf16[1,256,1536]{2,1,0:T(8,128)(2,1)}), bf16[1,2048,1536]{2,1,0:T(8,128)(2,1)}) %all-gather.17.cloned.1.call-update) | async-done | bytes 6291472 | tf_op jit(solution)/shard_map/all_gather | solution.py:19
  579.8 12.6 fusion.285
  592.4 9.8 convolution_convert_fusion.1
  605.7 10.1 convolution_convert_fusion.2
  615.8 61.4 %all-to-all-done.4 = bf16[1,8,256,1536]{3,2,0,1:T(8,128)(2,1)} async-done(((bf16[1,8,256,1536]{3,2,0,1:T(8,128)(2,1)}), bf16[1,8,256,1536]{3,2,0,1:T(8,128)(2,1)}, u32[]{:S(2)}, u32[]{:S(2)}) %all-to-all-start.4) | async-done | bytes 6291488 | tf_op jit(solution)/shard_map/all_to_all | solution.py:25
  688.1 64.0 %all-to-all-done.3 = bf16[1,8,256,1536]{3,2,0,1:T(8,128)(2,1)} async-done(((bf16[1,8,256,1536]{3,2,0,1:T(8,128)(2,1)}), bf16[1,8,256,1536]{3,2,0,1:T(8,128)(2,1)}, u32[]{:S(2)}, u32[]{:S(2)}) %all-to-all-start.3) | async-done | bytes 6291488 | tf_op jit(solution)/shard_map/all_to_all | solution.py:25
  760.1 38.7 %all-gather.19.cloned.1.call-done = bf16[1,2048,1536]{2,1,0:T(8,128)(2,1)} async-done(((bf16[1,256,1536]{2,1,0:T(8,128)(2,1)}), bf16[1,2048,1536]{2,1,0:T(8,128)(2,1)}) %all-gather.19.cloned.1.call-update) | async-done | bytes 6291472 | tf_op jit(solution)/shard_map/all_gather | solution.py:19
  804.8 12.3 convolution_convert_fusion.5
  817.0 14.6 %fusion.203 = f32[2,2048,2048]{1,2,0:T(8,128)} fusion(bf16[2048,2,96]{0,2,1:T(8,128)(2,1)} %fusion.116, f32[2048,2,96]{0,2,1:T(8,128)S(1)} %bitcast.419), kind=kOutput, calls=%fused_computation.257 | convolution fusion | flops 1611005952 | bytes 35913728 | tf_op jit(solution)/shard_map/bqhe,bkhe->bhqk/dot_general | solution.py:43
  831.7 33.2 %fusion.128 = bf16[2,96,2048]{2,1,0:T(8,128)(2,1)S(1)} fusion(bf16[2,2048,2048]{1,2,0:T(8,128)(2,1)} %copy-done.1, f32[2,2048,2048]{1,2,0:T(8,128)} %fusion.203, f32[2048,2,96]{0,2,1:T(8,128)} %bitcast.459), kind=kOutput, calls=%fused_computation.144 | convolution fusion | flops 1670125568 | bytes 52690944 | tf_op jit(solution)/shard_map/bhqk,bkhe->bqhe/dot_general | solution.py:47
  864.9 33.6 %fusion.129 = bf16[2,96,2048]{2,1,0:T(8,128)(2,1)S(1)} fusion(bf16[2,2048,2048]{1,2,0:T(8,128)(2,1)} %copy-done.1, f32[2,2048,2048]{1,2,0:T(8,128)} %fusion.203, f32[2048,2,96]{0,2,1:T(8,128)} %bitcast.457), kind=kOutput, calls=%fused_computation.145 | convolution fusion | flops 1670125568 | bytes 52690944 | tf_op jit(solution)/shard_map/bhqk,bqhe->bkhe/dot_general | solution.py:48
  899.4 7.5 fusion.180
  906.9 7.5 fusion.182
  914.3 9.4 fusion.19
  923.8 73.0 %all_to_all.42 = bf16[1,8,256,1536]{3,2,0,1:T(8,128)(2,1)S(1)} all-to-all(bf16[1,8,256,1536]{3,2,0,1:T(8,128)(2,1)S(1)} %bitcast.415), channel_id=1, replica_groups=mesh['dp'=1,'tp'=8] {'tp'}, dimensions={1} | all-to-all | bytes 12582912 | tf_op jit(solution)/shard_map/all_to_all | solution.py:25
  1002.4 38.7 %all-gather.21.cloned.1.call-done = bf16[1,2048,1536]{2,1,0:T(8,128)(2,1)} async-done(((bf16[1,256,1536]{2,1,0:T(8,128)(2,1)}), bf16[1,2048,1536]{2,1,0:T(8,128)(2,1)}) %all-gather.21.cloned.1.call-update) | async-done | bytes 6291472 | tf_op jit(solution)/shard_map/all_gather | solution.py:19
  1041.2 12.0 fusion.286
  1053.2 8.1 convolution_convert_fusion
  1061.3 73.0 %all_to_all.43 = bf16[1,8,256,1536]{3,2,0,1:T(8,128)(2,1)S(1)} all-to-all(bf16[1,8,256,1536]{3,2,0,1:T(8,128)(2,1)S(1)} %bitcast.425), channel_id=1, replica_groups=mesh['dp'=1,'tp'=8] {'tp'}, dimensions={1} | all-to-all | bytes 12582912 | tf_op jit(solution)/shard_map/all_to_all | solution.py:25
  1140.6 9.4 fusion.110
  1150.0 10.7 fusion.107
  1170.6 6.5 fusion.113
  1177.1 6.8 fusion.104
  1188.9 11.1 convolution_convert_fusion.4
  1200.0 13.1 fusion.206
  1213.2 34.0 %fusion.130 = bf16[2,96,2048]{2,1,0:T(8,128)(2,1)} fusion(bf16[2,2048,2048]{1,2,0:T(8,128)(2,1)} %copy-done, f32[2,2048,2048]{1,2,0:T(8,128)} %fusion.206, f32[2048,2,96]{0,2,1:T(8,128)} %bitcast.455), kind=kOutput, calls=%fused_computation.146 | convolution fusion | flops 1670125568 | bytes 52690944 | tf_op jit(solution)/shard_map/bhqk,bkhe->bqhe/dot_general | solution.py:47
  1247.1 34.6 %fusion.131 = bf16[2,96,2048]{2,1,0:T(8,128)(2,1)} fusion(bf16[2,2048,2048]{1,2,0:T(8,128)(2,1)} %copy-done, f32[2,2048,2048]{1,2,0:T(8,128)} %fusion.206, f32[2048,2,96]{0,2,1:T(8,128)} %bitcast.453), kind=kOutput, calls=%fused_computation.147 | convolution fusion | flops 1670125568 | bytes 52690944 | tf_op jit(solution)/shard_map/bhqk,bqhe->bkhe/dot_general | solution.py:48
  1281.8 7.6 fusion.185
  1289.4 6.3 fusion.187
  1295.7 12.1 fusion.18
  1333.9 48.9 %all-to-all-done.7 = bf16[1,8,256,1536]{3,2,0,1:T(8,128)(2,1)} async-done(((bf16[1,8,256,1536]{3,2,0,1:T(8,128)(2,1)}), bf16[1,8,256,1536]{3,2,0,1:T(8,128)(2,1)}, u32[]{:S(2)}, u32[]{:S(2)}) %all-to-all-start.7) | async-done | bytes 6291488 | tf_op jit(solution)/shard_map/all_to_all | solution.py:25
  1393.0 38.9 %all-reduce.3.cloned.1.call-done = (f32[2,4,1536]{2,1,0:T(4,128)}, f32[2,2,1536]{2,1,0:T(2,128)}) async-done(((f32[2,4,1536]{2,1,0:T(4,128)}, f32[2,2,1536]{2,1,0:T(2,128)}), (f32[2,4,1536]{2,1,0:T(4,128)}, f32[2,2,1536]{2,1,0:T(2,128)})) %all-reduce.3.cloned.1.call-update) | async-done | bytes 73744 | tf_op jit(solution)/shard_map/psum | solution.py:113
  (332 shorter events, 156.4 us)
Async XLA Ops:
  7.2 8.3 copy-start.27
  7.2 50.8 %all-gather.9.cloned.1.call-start = ((), (), s32[]{:S(2)}) async-start(), calls=%async_computation.8 | async-start | bytes 7077888 | tf_op jit(solution)/shard_map/all_gather | solution.py:19
  12.5 182.7 %copy-start.46 = (f32[1536]{0:T(1024)}, f32[1536]{0:T(1024)S(1)}, u32[]{:S(2)}) copy-start(f32[1536]{0:T(1024)S(1)} %get-tuple-element.31) | copy-start | bytes 18436
  12.5 314.6 %copy-start.48 = (f32[1536]{0:T(1024)}, f32[1536]{0:T(1024)S(1)}, u32[]{:S(2)}) copy-start(f32[1536]{0:T(1024)S(1)} %get-tuple-element.29) | copy-start | bytes 18436
  98.7 12.3 copy-start
  115.5 75.1 %all-to-all-start = ((bf16[1,8,256,1536]{3,2,0,1:T(8,128)(2,1)}), bf16[1,8,256,1536]{3,2,0,1:T(8,128)(2,1)}, u32[]{:S(2)}, u32[]{:S(2)}) async-start(bf16[1,8,256,1536]{3,2,0,1:T(8,128)(2,1)} %bitcast.412), calls=%async_computation | async-start | bytes 12582912 | tf_op jit(solution)/shard_map/all_to_all | solution.py:25
  119.1 75.4 %copy-start.4 = (bf16[1,256,1536]{2,1,0:T(8,128)(2,1)S(1)}, bf16[1,256,1536]{2,1,0:T(8,128)(2,1)}, u32[]{:S(2)}) copy-start(bf16[1,256,1536]{2,1,0:T(8,128)(2,1)} %param.9) | copy-start | bytes 2359300
  119.2 116.0 %all-gather.11.cloned.1.call-start = ((), (), s32[]{:S(2)}) async-start(), calls=%async_computation.9 | async-start | bytes 7077888 | tf_op jit(solution)/shard_map/all_gather | solution.py:19
  194.8 131.6 %copy-start.2 = (f32[1,256,1536]{2,1,0:T(8,128)}, f32[1,256,1536]{2,1,0:T(8,128)S(1)}, u32[]{:S(2)}) copy-start(f32[1,256,1536]{2,1,0:T(8,128)S(1)} %get-tuple-element.58) | copy-start | bytes 4718596
  194.8 48.4 %copy-start.57 = (f32[256]{0:T(256)}, f32[256]{0:T(256)S(1)}, u32[]{:S(2)}) copy-start(f32[256]{0:T(256)S(1)} %broadcast_multiply_fusion.2) | copy-start | bytes 3076
  195.1 48.1 %copy-start.70 = (f32[256]{0:T(256)}, f32[256]{0:T(256)S(1)}, u32[]{:S(2)}) copy-start(f32[256]{0:T(256)S(1)} %multiply_reduce_fusion.5) | copy-start | bytes 3076
  195.2 48.1 %copy-start.62 = (f32[256]{0:T(256)}, f32[256]{0:T(256)S(1)}, u32[]{:S(2)}) copy-start(f32[256]{0:T(256)S(1)} %fusion.210) | copy-start | bytes 3076
  196.4 170.7 %all-gather.13.cloned.1.call-start = ((), (), s32[]{:S(2)}) async-start(), calls=%async_computation.10 | async-start | bytes 7077888 | tf_op jit(solution)/shard_map/all_gather | solution.py:19
  196.5 46.8 %copy-start.75 = (f32[768]{0:T(1024)}, f32[768]{0:T(1024)S(1)}, u32[]{:S(2)}) copy-start(f32[768]{0:T(1024)S(1)} %get-tuple-element.40) | copy-start | bytes 9220
  243.3 9.4 copy-start.84
  326.7 40.4 %copy-start.42 = (bf16[1536,1,2,96]{0,3,2,1:T(8,128)(2,1)S(1)}, bf16[1536,1,2,96]{0,3,2,1:T(8,128)(2,1)}, u32[]{:S(2)}) copy-start(bf16[1536,1,2,96]{0,3,2,1:T(8,128)(2,1)} %get-tuple-element.64) | copy-start | bytes 1769476
  326.7 46.7 %copy-start.59 = (f32[256]{0:T(256)}, f32[256]{0:T(256)S(1)}, u32[]{:S(2)}) copy-start(f32[256]{0:T(256)S(1)} %broadcast_multiply_fusion.1) | copy-start | bytes 3076
  327.0 46.4 %copy-start.72 = (f32[256]{0:T(256)}, f32[256]{0:T(256)S(1)}, u32[]{:S(2)}) copy-start(f32[256]{0:T(256)S(1)} %multiply_reduce_fusion.4) | copy-start | bytes 3076
  327.1 46.4 %copy-start.64 = (f32[256]{0:T(256)}, f32[256]{0:T(256)S(1)}, u32[]{:S(2)}) copy-start(f32[256]{0:T(256)S(1)} %fusion.211) | copy-start | bytes 3076
  328.4 210.2 %all-gather.15.cloned.1.call-start = ((), (), s32[]{:S(2)}) async-start(), calls=%async_computation.11 | async-start | bytes 7077888 | tf_op jit(solution)/shard_map/all_gather | solution.py:19
  397.1 12.7 copy-start.40
  409.8 12.4 copy-start.1
  499.8 80.0 %all-gather.17.cloned.1.call-start = ((), (), s32[]{:S(2)}) async-start(), calls=%async_computation.12 | async-start | bytes 7077888 | tf_op jit(solution)/shard_map/all_gather | solution.py:19
  592.4 9.8 copy-start.81
  602.2 75.0 %all-to-all-start.4 = ((bf16[1,8,256,1536]{3,2,0,1:T(8,128)(2,1)}), bf16[1,8,256,1536]{3,2,0,1:T(8,128)(2,1)}, u32[]{:S(2)}, u32[]{:S(2)}) async-start(bf16[1,8,256,1536]{3,2,0,1:T(8,128)(2,1)} %bitcast.423), calls=%async_computation.4 | async-start | bytes 12582912 | tf_op jit(solution)/shard_map/all_to_all | solution.py:25
  677.2 75.0 %all-to-all-start.3 = ((bf16[1,8,256,1536]{3,2,0,1:T(8,128)(2,1)}), bf16[1,8,256,1536]{3,2,0,1:T(8,128)(2,1)}, u32[]{:S(2)}, u32[]{:S(2)}) async-start(bf16[1,8,256,1536]{3,2,0,1:T(8,128)(2,1)} %bitcast.422), calls=%async_computation.3 | async-start | bytes 12582912 | tf_op jit(solution)/shard_map/all_to_all | solution.py:25
  680.7 118.1 %all-gather.19.cloned.1.call-start = ((), (), s32[]{:S(2)}) async-start(), calls=%async_computation.13 | async-start | bytes 7077888 | tf_op jit(solution)/shard_map/all_gather | solution.py:19
  688.1 68.0 %copy-start.56 = (f32[1536]{0:T(1024)S(1)}, f32[1536]{0:T(1024)}, u32[]{:S(2)}) copy-start(f32[1536]{0:T(1024)} %get-tuple-element.35) | copy-start | bytes 18436
  760.1 281.1 %all-gather.21.cloned.1.call-start = ((), (), s32[]{:S(2)}) async-start(), calls=%async_computation.14 | async-start | bytes 7077888 | tf_op jit(solution)/shard_map/all_gather | solution.py:19
  804.8 12.3 copy-start.9
  864.9 42.0 %copy-start.35 = (bf16[2,96,2048]{2,1,0:T(8,128)(2,1)}, bf16[2,96,2048]{2,1,0:T(8,128)(2,1)S(1)}, u32[]{:S(2)}) copy-start(bf16[2,96,2048]{2,1,0:T(8,128)(2,1)S(1)} %fusion.128) | copy-start | bytes 2359300
  1000.5 40.7 %copy-start.76 = (f32[768]{0:T(1024)S(1)}, f32[768]{0:T(1024)}, u32[]{:S(2)}) copy-start(f32[768]{0:T(1024)} %copy-done.75) | copy-start | bytes 9220
  1002.4 181.5 %all-gather.23.cloned.1.call-start = ((), (), s32[]{:S(2)}) async-start(), calls=%async_computation.15 | async-start | bytes 7077888 | tf_op jit(solution)/shard_map/all_gather | solution.py:19
  1140.6 20.3 %slice-start.4 = ((s8[6291456]{0:T(1024)(128)(4,1)}), s8[4194304]{0:T(1024)(128)(4,1)S(1)}, s32[]{:S(2)}) async-start(s8[6291456]{0:T(1024)(128)(4,1)} %bitcast.446), calls=%async_computation.21 | async-start | bytes 8388608
  1150.0 10.8 copy-start.26
  1150.0 10.9 slice-start.5
  1167.4 9.6 slice-start.8
  1167.4 9.6 slice-start.10
  1188.9 11.2 copy-start.7
  1247.1 34.6 %copy-start.11 = (bf16[1536,3,2,96]{0,3,2,1:T(8,128)(2,1)S(1)}, bf16[1536,3,2,96]{0,3,2,1:T(8,128)(2,1)}, u32[]{:S(2)}) copy-start(bf16[1536,3,2,96]{0,3,2,1:T(8,128)(2,1)} %copy-done.10) | copy-start | bytes 5308420
  1307.9 75.0 %all-to-all-start.7 = ((bf16[1,8,256,1536]{3,2,0,1:T(8,128)(2,1)}), bf16[1,8,256,1536]{3,2,0,1:T(8,128)(2,1)}, u32[]{:S(2)}, u32[]{:S(2)}) async-start(bf16[1,8,256,1536]{3,2,0,1:T(8,128)(2,1)} %bitcast.414), calls=%async_computation.7 | async-start | bytes 12582912 | tf_op jit(solution)/shard_map/all_to_all | solution.py:25
  1311.4 120.6 %all-reduce.3.cloned.1.call-start = ((), (), s32[]{:S(2)}) async-start(), calls=%async_computation.16 | async-start | bytes 147456 | tf_op jit(solution)/shard_map/psum | solution.py:113
  1317.2 8.8 slice-start
  1333.9 54.4 %copy-start.5 = (bf16[1,256,1536]{2,1,0:T(8,128)(2,1)S(1)}, bf16[1,256,1536]{2,1,0:T(8,128)(2,1)}, u32[]{:S(2)}) copy-start(bf16[1,256,1536]{2,1,0:T(8,128)(2,1)} %param.9) | copy-start | bytes 2359300
  1333.9 54.4 %copy-start.45 = (f32[1536]{0:T(1024)S(1)}, f32[1536]{0:T(1024)}, u32[]{:S(2)}) copy-start(f32[1536]{0:T(1024)} %copy-done.44) | copy-start | bytes 18436
  1333.9 54.4 %copy-start.52 = (f32[256]{0:T(256)S(1)}, f32[256]{0:T(256)}, u32[]{:S(2)}) copy-start(f32[256]{0:T(256)} %copy-done.51) | copy-start | bytes 3076
  1333.9 54.8 %copy-start.69 = (f32[256]{0:T(256)S(1)}, f32[256]{0:T(256)}, u32[]{:S(2)}) copy-start(f32[256]{0:T(256)} %copy-done.68) | copy-start | bytes 3076
  1333.9 54.8 %copy-start.67 = (f32[256]{0:T(256)S(1)}, f32[256]{0:T(256)}, u32[]{:S(2)}) copy-start(f32[256]{0:T(256)} %copy-done.66) | copy-start | bytes 3076
  (62 other events, 191.6 us)
Sparse Core Ops, SparseCore 0:
  15.6 42.3 all-gather.8
  196.6 38.5 all-gather.10
  328.5 38.6 all-gather.12
  499.9 38.6 all-gather.14
  540.2 39.5 all-gather.16
  760.2 38.5 all-gather.18
  1002.5 38.6 all-gather.20
  1140.7 38.6 all-gather.22
  1390.3 41.5 all-reduce.2
where the time goes:
time: 1450 us; the launch traced here: 1440 us
  waiting for transfers between devices  544 us (38%)
  matrix products  465 us (32%)
  blocking collectives  292 us (20%)
  other arithmetic  92.9 us (6%)
  local copies, waits for them, and re-layouts  17.5 us (1%)
  between operations  15.7 us (1%)
  starting transfers between devices  14.7 us (1%)
    all_to_all x4, blocking collectives, scatter_rows(): received = lax.all_to_all(sent, 'tp', 1, 1, tiled=True)  292 us
    all_gather x8, waiting for transfers between devices, gather_rows(): return lax.all_gather(local_vals, 'tp', axis=1, tiled=True)  260 us
    all_to_all x4, waiting for transfers between devices, scatter_rows(): received = lax.all_to_all(sent, 'tp', 1, 1, tiled=True)  245 us
    dot_general x2, matrix products, attention_backward(): jnp.einsum('bhqk,bqhe->bkhe', d_score, q_vals, preferred_element_type=jnp...  68.2 us
    dot_general x2, matrix products, attention_backward(): jnp.einsum('bhqk,bkhe->bqhe', d_score, k_vals, preferred_element_type=jnp...  67.2 us
    unnamed x12, matrix products  45.6 us
    sub x2, matrix products, causal_attention(): prob_bf = jax.nn.softmax(scores, axis=-1).astype(jnp.bfloat16)  39.8 us
    psum x1, waiting for transfers between devices, device_step(): lax.psum((jnp.stack([grad_set[0] for grad_set in layer_grads]), jnp.stack...  38.9 us
  transfers between devices with their start and end apart: 13, of which 12 were waited for; matrix products, arithmetic and copies ran while one was open for 7% of the time, Pallas kernels for 0%

commit v1 on v0

v1 whole, which is shorter than its diff:
```python
import functools
import math

import jax
import jax.numpy as jnp
from jax import lax
from jax.experimental import pallas as pl
from jax.experimental.pallas import tpu as pltpu
from jax.sharding import PartitionSpec as P

MESH = pl.DeviceIdType.MESH
BF16 = jnp.bfloat16
F32 = jnp.float32
LOG2E = math.log2(math.e)
VMEM_LIMIT = 60 * 1024 * 1024
LANES = 128


def dot_nn(a, b):
    return lax.dot_general(a, b, (((1,), (0,)), ((), ())), preferred_element_type=F32)


def dot_nt(a, b):
    return lax.dot_general(a, b, (((1,), (1,)), ((), ())), preferred_element_type=F32)


def dot_tn(a, b):
    return lax.dot_general(a, b, (((0,), (0,)), ((), ())), preferred_element_type=F32)


def attn_fwd_kernel(scale, n_q, q_ref, k_ref, v_ref, a_ref, lse_ref):
    blk = q_ref.shape[0]
    coef = scale * LOG2E
    row = lax.broadcasted_iota(jnp.int32, (blk, blk), 0)
    col = lax.broadcasted_iota(jnp.int32, (blk, blk), 1)

    def variant(i):
        q = q_ref[...]
        parts = []
        for j in range(i + 1):
            s = dot_nt(q, k_ref[j * blk:(j + 1) * blk, :])
            if j == i:
                s = jnp.where(row >= col, s, -1e30)
            parts.append(s)
        top = parts[0]
        for s in parts[1:]:
            top = jnp.maximum(top, s)
        top = jnp.max(top, axis=-1, keepdims=True) * coef
        parts = [jnp.exp2(s * coef - top) for s in parts]
        total = parts[0]
        for e in parts[1:]:
            total = total + e
        total = jnp.sum(total, axis=-1, keepdims=True)
        inv = 1.0 / total
        out = None
        for j, e in enumerate(parts):
            o = dot_nn((e * inv).astype(BF16), v_ref[j * blk:(j + 1) * blk, :])
            out = o if out is None else out + o
        a_ref[...] = out.astype(BF16)
        lse = jnp.broadcast_to(top + jnp.log2(total), (blk, 128))
        lse_ref[0] = jnp.transpose(lse)[0:1, :]

    for i in range(n_q):
        pl.when(pl.program_id(1) == i)(functools.partial(variant, i))


def attention_forward(qkv, head_dim, n_heads):
    seq = qkv.shape[0]
    blk = 512
    n_q = seq // blk
    return pl.pallas_call(
        functools.partial(attn_fwd_kernel, head_dim ** -0.5, n_q),
        grid=(n_heads, n_q),
        in_specs=[pl.BlockSpec((blk, 128), lambda h, i: (i, h)),
                  pl.BlockSpec((seq, 128), lambda h, i: (0, n_heads + h)),
                  pl.BlockSpec((seq, 128), lambda h, i: (0, 2 * n_heads + h))],
        out_specs=[pl.BlockSpec((blk, 128), lambda h, i: (i, h)),
                   pl.BlockSpec((1, 1, blk), lambda h, i: (h, 0, i))],
        out_shape=[jax.ShapeDtypeStruct((seq, n_heads * 128), BF16),
                   jax.ShapeDtypeStruct((n_heads, 1, seq), F32)],
        compiler_params=pltpu.CompilerParams(dimension_semantics=("arbitrary", "arbitrary"), vmem_limit_bytes=40 * 1024 * 1024),
        cost_estimate=pl.CostEstimate(flops=4 * seq * seq * 128, bytes_accessed=8 * seq * 256, transcendentals=seq * seq),
        name="attn_fwd",
    )(qkv, qkv, qkv)


def attn_bwd_kernel(scale, n_q, q_ref, k_ref, v_ref, a_ref, da_ref, lse_ref, dq_ref, dk_ref, dv_ref, dk_acc, dv_acc):
    blk = q_ref.shape[0]
    coef = scale * LOG2E
    key = lax.broadcasted_iota(jnp.int32, (blk, blk), 0)
    qry = lax.broadcasted_iota(jnp.int32, (blk, blk), 1)

    def variant(i):
        q = q_ref[...]
        da = da_ref[...]
        lse = lse_ref[0]
        row_dot = jnp.sum(jnp.transpose(da.astype(F32) * a_ref[...].astype(F32)), axis=0, keepdims=True)
        dq = None
        for j in range(i, -1, -1):
            rows = slice(j * blk, (j + 1) * blk)
            k = k_ref[rows, :]
            p = jnp.exp2(dot_nt(k, q) * coef - lse)
            if j == i:
                p = jnp.where(qry >= key, p, 0.0)
            dv = dot_nn(p.astype(BF16), da)
            ds = (p * (dot_nt(v_ref[rows, :], da) - row_dot)).astype(BF16)
            dk = dot_nn(ds, q)
            if j == i:
                dv_acc[rows, :] = dv
                dk_acc[rows, :] = dk
            else:
                dv_acc[rows, :] += dv
                dk_acc[rows, :] += dk
            d = dot_tn(ds, k)
            dq = d if dq is None else dq + d
        dq_ref[...] = (dq * scale).astype(BF16)

    for i in range(n_q):
        pl.when(pl.program_id(1) == i)(functools.partial(variant, i))

    @pl.when(pl.program_id(1) == n_q - 1)
    def _():
        dk_ref[...] = (dk_acc[...] * scale).astype(BF16)
        dv_ref[...] = dv_acc[...].astype(BF16)


def attention_backward(qkv, attn, d_attn, lse, head_dim, n_heads):
    seq = qkv.shape[0]
    blk = 512
    n_q = seq // blk
    row = pl.BlockSpec((blk, 128), lambda h, i: (i, h))
    full = pl.BlockSpec((seq, 128), lambda h, i: (0, h))
    shape = jax.ShapeDtypeStruct((seq, n_heads * 128), BF16)
    return pl.pallas_call(
        functools.partial(attn_bwd_kernel, head_dim ** -0.5, n_q),
        grid=(n_heads, n_q),
        in_specs=[row,
                  pl.BlockSpec((seq, 128), lambda h, i: (0, n_heads + h)),
                  pl.BlockSpec((seq, 128), lambda h, i: (0, 2 * n_heads + h)),
                  row, row,
                  pl.BlockSpec((1, 1, blk), lambda h, i: (h, 0, i))],
        out_specs=[row, full, full],
        out_shape=[shape, shape, shape],
        scratch_shapes=[pltpu.VMEM((seq, 128), F32), pltpu.VMEM((seq, 128), F32)],
        compiler_params=pltpu.CompilerParams(dimension_semantics=("arbitrary", "arbitrary"), vmem_limit_bytes=40 * 1024 * 1024),
        cost_estimate=pl.CostEstimate(flops=10 * seq * seq * 128, bytes_accessed=16 * seq * 256, transcendentals=seq * seq),
        name="attn_bwd",
    )(qkv, qkv, qkv, attn, d_attn, lse)


class Place:
    def __init__(self):
        t = lax.axis_index("tp")
        self.me = t
        self.dc = 1 - 2 * (t % 2)
        self.dx = 2 - 4 * ((t // 2) % 2)
        self.dy = 4 - 8 * (t // 4)
        self.partner = t + self.dc
        self.xn = t + self.dx
        self.yn = t + self.dy


def barrier(pos):
    sem = pltpu.get_barrier_semaphore()
    for peer in (pos.partner, pos.xn, pos.yn):
        pl.semaphore_signal(sem, inc=1, device_id={"tp": peer}, device_id_type=MESH)
    pl.semaphore_wait(sem, 3)


def rdma(src, dst, sems, idx, peer):
    send, recv = sems
    return pltpu.make_async_remote_copy(src_ref=src, dst_ref=dst, send_sem=send.at[idx], recv_sem=recv.at[idx],
                                        device_id={"tp": peer}, device_id_type=MESH)


def rs_scratch(rows, width):
    half = rows // 2
    return dict(
        rs_snd=pltpu.VMEM((4, rows, width), BF16), rs_rcv=pltpu.VMEM((4, rows, width), BF16),
        rs_sum=pltpu.VMEM((4, rows, width), F32), rs_out=pltpu.VMEM((3, rows, width), BF16),
        rs_in=pltpu.VMEM((6, half, width), BF16),
        rs_psend=pltpu.SemaphoreType.DMA((4,)), rs_precv=pltpu.SemaphoreType.DMA((4,)),
        rs_send=pltpu.SemaphoreType.DMA((6,)), rs_recv=pltpu.SemaphoreType.DMA((6,)))


def reduce_scatter(pos, r, produce, rows, width, n_chunk=3):
    half = rows // 2
    top, low = pl.ds(0, half), pl.ds(half, half)
    wide = width // n_chunk
    psem = (r.rs_psend, r.rs_precv)
    isem = (r.rs_send, r.rs_recv)

    def dest(k):
        return pos.me + (1 - k // 2) * pos.dx + (1 - k % 2) * pos.dy

    def to_partner(k):
        return rdma(r.rs_snd.at[k], r.rs_rcv.at[k], psem, k, pos.partner)

    def first(k, carry):
        block = dest(k) + pos.dc
        for c in range(n_chunk):
            cols = pl.ds(c * wide, wide)
            r.rs_snd[k, :, cols] = produce(block, cols).astype(BF16)
        to_partner(k).start()
        return carry

    lax.fori_loop(0, 4, first, 0)

    diag_x = rdma(r.rs_out.at[0, top], r.rs_in.at[0], isem, 0, pos.xn)
    diag_y = rdma(r.rs_out.at[0, low], r.rs_in.at[1], isem, 1, pos.yn)
    x_top = rdma(r.rs_out.at[1, top], r.rs_in.at[2], isem, 2, pos.xn)
    x_low = rdma(r.rs_out.at[1, low], r.rs_in.at[3], isem, 3, pos.xn)
    y_top = rdma(r.rs_out.at[2, top], r.rs_in.at[4], isem, 4, pos.yn)
    y_low = rdma(r.rs_out.at[2, low], r.rs_in.at[5], isem, 5, pos.yn)

    def second(k, carry):
        block = dest(k)
        to_partner(k).wait_recv()
        for c in range(n_chunk):
            cols = pl.ds(c * wide, wide)
            total = produce(block, cols) + r.rs_rcv[k, :, cols].astype(F32)
            r.rs_sum[k, :, cols] = total

            @pl.when(k < 3)
            def _():
                r.rs_out[k, :, cols] = r.rs_sum[k, :, cols].astype(BF16)

        @pl.when(k == 0)
        def _():
            diag_x.start()
            diag_y.start()

        @pl.when(k == 1)
        def _():
            x_top.start()

        @pl.when(k == 2)
        def _():
            y_low.start()

        return carry

    lax.fori_loop(0, 4, second, 0)

    diag_y.wait_recv()
    diag_x.wait_recv()

    def add_relay(slot, src, part):
        def body(i, carry):
            rr = pl.ds(pl.multiple_of(i * 16, 16), 16)
            at = pl.ds(pl.multiple_of(part * half + i * 16, 16), 16)
            r.rs_out[slot, at, :] = (r.rs_sum[slot, at, :] + r.rs_in[src, rr, :].astype(F32)).astype(BF16)
            return carry

        lax.fori_loop(0, half // 16, body, 0)

    add_relay(2, 0, 0)
    y_top.start()
    add_relay(1, 1, 1)
    x_low.start()

    x_top.wait_recv()
    y_low.wait_recv()
    y_top.wait_recv()
    x_low.wait_recv()

    def finish():
        for k in range(4):
            to_partner(k).wait_send()
        for copy in (diag_x, diag_y, x_top, x_low, y_top, y_low):
            copy.wait_send()

    return finish


def rs_rows(r, half, start, count):
    at = pl.ds(start, count)
    part = start // half
    inner = pl.ds(pl.multiple_of(start - part * half, count), count)
    return (r.rs_sum[3, at, :] + r.rs_in[2 + part, inner, :].astype(F32)) + r.rs_in[4 + part, inner, :].astype(F32)


def ag_scratch(seq, width):
    return dict(h_vm=pltpu.VMEM((seq, width), BF16),
                ag_send=pltpu.SemaphoreType.DMA((13,)), ag_recv=pltpu.SemaphoreType.DMA((13,)),
                h_out=pltpu.SemaphoreType.DMA((8,)))


def all_gather(pos, r, consume, rows, h_hbm, streams):
    half = rows // 2
    sems = (r.ag_send, r.ag_recv)

    def piece(owner, part):
        return r.h_vm.at[pl.ds(pl.multiple_of(owner * rows + part * half, half), half)]

    def whole(owner):
        return r.h_vm.at[pl.ds(pl.multiple_of(owner * rows, rows), rows)]

    def copy(ref, idx, peer):
        return rdma(ref, ref, sems, idx, peer)

    me, xn, yn = pos.me, pos.xn, pos.yn
    dn = me + pos.dx + pos.dy
    own_p = copy(whole(me), 0, pos.partner)
    own_xa = copy(piece(me, 0), 1, xn)
    own_xb = copy(piece(me, 1), 2, xn)
    own_ya = copy(piece(me, 0), 3, yn)
    own_yb = copy(piece(me, 1), 4, yn)
    relay_y = copy(piece(xn, 0), 5, yn)
    relay_x = copy(piece(yn, 1), 6, xn)
    fwd_xa = copy(piece(xn, 0), 7, pos.partner)
    fwd_xb = copy(piece(xn, 1), 8, pos.partner)
    fwd_ya = copy(piece(yn, 0), 9, pos.partner)
    fwd_yb = copy(piece(yn, 1), 10, pos.partner)
    fwd_da = copy(piece(dn, 0), 11, pos.partner)
    fwd_db = copy(piece(dn, 1), 12, pos.partner)
    own_xa.start()
    own_yb.start()
    own_xb.start()
    own_ya.start()
    own_p.start()

    def out_copies(s, block):
        at = pl.ds(pl.multiple_of(block * rows, rows), rows)
        made = [pltpu.make_async_copy(r.h_vm.at[at], h_hbm.at[at], r.h_out.at[s])]
        for src, dst, sem in streams:
            made.append(pltpu.make_async_copy(src.at[at], dst.at[at], sem.at[s]))
        return made

    def block_of(s):
        return me + (s % 2) * pos.dc + ((s // 2) % 2) * pos.dx + (s // 4) * pos.dy

    def step(s, carry):
        @pl.when(s == 1)
        def _():
            own_p.wait_recv()

        @pl.when(s == 2)
        def _():
            own_xa.wait_recv()
            relay_y.start()
            fwd_xa.start()
            own_yb.wait_recv()
            relay_x.start()
            fwd_yb.start()
            own_xb.wait_recv()
            fwd_xb.start()

        @pl.when(s == 3)
        def _():
            own_ya.wait_recv()
            fwd_ya.start()
            fwd_xa.wait_recv()
            fwd_xb.wait_recv()

        @pl.when(s == 5)
        def _():
            fwd_ya.wait_recv()
            fwd_yb.wait_recv()

        @pl.when(s == 6)
        def _():
            relay_y.wait_recv()
            fwd_da.start()
            relay_x.wait_recv()
            fwd_db.start()

        @pl.when(s == 7)
        def _():
            fwd_da.wait_recv()
            fwd_db.wait_recv()

        block = block_of(s)
        consume(block)
        for c in out_copies(s, block):
            c.start()
        return carry

    lax.fori_loop(0, 8, step, 0)

    def finish():
        for c in (own_p, own_xa, own_xb, own_ya, own_yb, relay_y, relay_x, fwd_xa, fwd_xb, fwd_ya, fwd_yb, fwd_da, fwd_db):
            c.wait_send()

        def drain(s, carry):
            for c in out_copies(s, block_of(s)):
                c.wait()
            return carry

        lax.fori_loop(0, 8, drain, 0)

    return finish


class Refs:
    pass


def comm_call(body, ins, outs, scratch, cid, name, flops):
    in_names, out_names, scr_names = list(ins), list(outs), list(scratch)
    any_spec, vmem_spec = pl.BlockSpec(memory_space=pl.ANY), pl.BlockSpec(memory_space=pltpu.VMEM)
    arrays, in_specs = [], []
    for key in in_names:
        val = ins[key]
        in_specs.append(any_spec if isinstance(val, tuple) else vmem_spec)
        arrays.append(val[0] if isinstance(val, tuple) else val)

    def kernel(*refs):
        r = Refs()
        for key, ref in zip(in_names + out_names + scr_names, refs):
            setattr(r, key, ref)
        body(r)

    result = pl.pallas_call(
        kernel,
        in_specs=in_specs,
        out_specs=[any_spec if outs[key][2] else vmem_spec for key in out_names],
        out_shape=[jax.ShapeDtypeStruct(outs[key][0], outs[key][1]) for key in out_names],
        scratch_shapes=[scratch[key] for key in scr_names],
        compiler_params=pltpu.CompilerParams(collective_id=cid, has_side_effects=True, vmem_limit_bytes=VMEM_LIMIT),
        cost_estimate=pl.CostEstimate(flops=flops, bytes_accessed=30_000_000, transcendentals=0),
        name=name,
    )(*arrays)
    return dict(zip(out_names, result))


def fold8(vals):
    out = vals[0:8]
    for i in range(8, vals.shape[0], 8):
        out = out + vals[i:i + 8]
    return out


def unit(cid, name, seq, width, *, lhs=None, weight=None, weight_t=False, local=None, local_in=None, tail=None, consume=None,
         cons_in=None, cons_out=None, cons_acc=None):
    rows = seq // 8
    half = rows // 2
    lhs, weight = lhs or [], weight or []
    cons_in, cons_out, cons_acc = cons_in or {}, cons_out or {}, cons_acc or {}
    ins, scratch, outs = {}, {}, {}
    loads = []
    for i, (a, w) in enumerate(zip(lhs, weight)):
        for tag, arr in ((f"lhs{i}", a), (f"w{i}", w)):
            ins[tag + "_h"] = (arr,)
            scratch[tag] = pltpu.VMEM(arr.shape, arr.dtype)
            loads.append(tag)
    n_prod = len(loads)
    for tag, arr in cons_in.items():
        ins[tag + "_h"] = (arr,)
        scratch[tag] = pltpu.VMEM(arr.shape, arr.dtype)
        loads.append(tag)
    ins.update(local_in or {})
    for tag, (shape, dtype) in (tail or {}).items():
        outs[tag] = (shape, dtype, False)
    if lhs:
        scratch.update(rs_scratch(rows, width))
    if consume:
        scratch.update(ag_scratch(seq, width))
        outs["h_all"] = ((seq, width), BF16, True)
        for tag, (cols, dtype) in cons_out.items():
            outs[tag + "_h"] = ((seq, cols), dtype, True)
            scratch[tag] = pltpu.VMEM((seq, cols), dtype)
            scratch[tag + "_s"] = pltpu.SemaphoreType.DMA((8,))
        for tag, (shape, dtype) in cons_acc.items():
            outs[tag] = (shape, dtype, False)
    scratch["load_sem"] = pltpu.SemaphoreType.DMA((max(len(loads), 1),))

    def body(r):
        pos = Place()
        load = [pltpu.make_async_copy(getattr(r, tag + "_h"), getattr(r, tag), r.load_sem.at[i]) for i, tag in enumerate(loads)]
        for c in load:
            c.start()
        barrier(pos)
        finish_rs = None
        get_rows = None
        if lhs:
            for c in load[:n_prod]:
                c.wait()

            def produce(block, cols):
                at = pl.ds(pl.multiple_of(block * rows, rows), rows)
                total = None
                for i in range(len(lhs)):
                    a, w = getattr(r, f"lhs{i}"), getattr(r, f"w{i}")
                    part = dot_nt(a[at, :], w[cols, :]) if weight_t else dot_nn(a[at, :], w[:, cols])
                    total = part if total is None else total + part
                return total

            finish_rs = reduce_scatter(pos, r, produce, rows, width)
            get_rows = functools.partial(rs_rows, r, half)
        local(r, pos, get_rows)
        if consume:
            for c in load[n_prod:]:
                c.wait()
            for tag in cons_acc:
                ref = getattr(r, tag)
                ref[...] = jnp.zeros_like(ref)
            streams = [(getattr(r, tag), getattr(r, tag + "_h"), getattr(r, tag + "_s")) for tag in cons_out]

            def run(block):
                consume(r, pl.ds(pl.multiple_of(block * rows, rows), rows))

            finish_ag = all_gather(pos, r, run, rows, r.h_all, streams)
            finish_ag()
        if finish_rs:
            finish_rs()

    flops = 2 * seq * width * (sum(a.shape[1] for a in lhs) + sum(c for c, _ in cons_out.values())) + 100_000
    if "small" in (local_in or {}):
        scratch.update(sm_rcv=pltpu.VMEM((3,) + local_in["small"].shape, F32), sm_snd=pltpu.VMEM((3,) + local_in["small"].shape, F32),
                       sm_send=pltpu.SemaphoreType.DMA((3,)), sm_recv=pltpu.SemaphoreType.DMA((3,)))
    return comm_call(body, ins, outs, scratch, cid, name, flops)


STEP_ROWS = 16


def normalize(res):
    mean = jnp.mean(res, axis=-1, keepdims=True)
    centered = res - mean
    var = jnp.mean(centered * centered, axis=-1, keepdims=True)
    rstd = lax.rsqrt(var + 1e-5)
    return centered * rstd, rstd


def local_forward(rows, with_sum, with_h):
    def run(r, pos, get_rows):
        base = pos.me * rows

        def step(i, carry):
            at = pl.multiple_of(i * STEP_ROWS, STEP_ROWS)
            here = pl.ds(at, STEP_ROWS)
            res = r.res[here, :].astype(F32)
            if with_sum:
                res = (res + get_rows(at, STEP_ROWS)) + r.ln[2:, :]
                r.res_out[here, :] = res.astype(r.res_out.dtype)
            if with_h:
                xhat, _ = normalize(res)
                r.h_vm[pl.ds(pl.multiple_of(base + at, STEP_ROWS), STEP_ROWS), :] = (
                    xhat * r.ln[0:1, :] + r.ln[1:2, :]).astype(BF16)
            return carry

        lax.fori_loop(0, rows // STEP_ROWS, step, 0)

    return run


def local_backward(rows, last, n_small=0):
    def run(r, pos, get_rows):
        base = pos.me * rows
        width = r.ln.shape[-1]

        def step(i, carry):
            d_gain, d_shift, d_bias = carry
            at = pl.multiple_of(i * STEP_ROWS, STEP_ROWS)
            here = pl.ds(at, STEP_ROWS)
            d_h = get_rows(at, STEP_ROWS)
            xhat, rstd = normalize(r.res[here, :].astype(F32))
            d_gain = d_gain + fold8(d_h * xhat)
            d_shift = d_shift + fold8(d_h)
            d_hat = d_h * r.ln[0:1, :]
            m_one = jnp.mean(d_hat, axis=-1, keepdims=True)
            m_two = jnp.mean(d_hat * xhat, axis=-1, keepdims=True)
            d_out = r.d_res[here, :].astype(F32) + rstd * (d_hat - m_one - xhat * m_two)
            d_bias = d_bias + fold8(d_out)
            r.d_out[here, :] = d_out.astype(r.d_out.dtype)
            if not last:
                r.h_vm[pl.ds(pl.multiple_of(base + at, STEP_ROWS), STEP_ROWS), :] = d_out.astype(BF16)
            return d_gain, d_shift, d_bias

        zero = jnp.zeros((8, width), F32)
        d_gain, d_shift, d_bias = lax.fori_loop(0, rows // STEP_ROWS, step, (zero, zero, zero))
        if not last:
            r.sums[0:1, :] = jnp.sum(d_gain, axis=0, keepdims=True)
            r.sums[1:2, :] = jnp.sum(d_shift, axis=0, keepdims=True)
            r.sums[2:3, :] = jnp.sum(d_bias, axis=0, keepdims=True)
            return
        r.sm_snd[0] = r.small[...]
        r.sm_snd[0, 0:1, :] = jnp.sum(d_gain, axis=0, keepdims=True)
        r.sm_snd[0, 1:2, :] = jnp.sum(d_shift, axis=0, keepdims=True)
        sems = (r.sm_send, r.sm_recv)
        copies = []
        for i, peer in enumerate((pos.partner, pos.xn, pos.yn)):
            c = rdma(r.sm_snd.at[i], r.sm_rcv.at[i], sems, i, peer)
            c.start()
            c.wait_recv()
            copies.append(c)
            total = r.sm_snd[i] + r.sm_rcv[i]
            if i < 2:
                r.sm_snd[i + 1] = total
            else:
                r.small_out[...] = total
        for c in copies:
            c.wait_send()

    return run


GELU_C = math.sqrt(2.0 / math.pi)


def gelu_pair(x):
    sq = x * x
    t = jnp.tanh(GELU_C * x * (1.0 + 0.044715 * sq))
    half = 0.5 * (1.0 + t)
    grad = half + (0.5 * GELU_C) * x * (1.0 - t * t) * (1.0 + (3 * 0.044715) * sq)
    return x * half, grad


def consume_qkv(r, at):
    h = r.h_vm[at, :]
    for c in range(0, r.qkv.shape[1], 256):
        cols = pl.ds(c, 256)
        r.qkv[at, cols] = dot_nt(h, r.wqkv[cols, :]).astype(BF16)


def consume_up(r, at):
    h = r.h_vm[at, :]
    for c in range(0, r.act.shape[1], 256):
        cols = pl.ds(c, 256)
        act, grad = gelu_pair(dot_nn(h, r.w_up[:, cols]) + r.b_up[:, cols])
        r.act[at, cols] = act.astype(BF16)
        r.gel[at, cols] = grad


def consume_up_down(r, at):
    h = r.h_vm[at, :]
    dy = r.dy[at, :]
    for c in range(0, r.act.shape[1], 256):
        cols = pl.ds(c, 256)
        act, grad = gelu_pair(dot_nn(h, r.w_up[:, cols]) + r.b_up[:, cols])
        r.act[at, cols] = act.astype(BF16)
        d_pre = dot_nt(dy, r.w_down[cols, :]) * grad
        r.d_bup[:, cols] += fold8(d_pre)
        r.d_pre[at, cols] = d_pre.astype(BF16)


def consume_dpre(r, at):
    d = r.h_vm[at, :]
    for c in range(0, r.d_pre.shape[1], 256):
        cols = pl.ds(c, 256)
        d_pre = dot_nt(d, r.w_down[cols, :]) * r.gel[at, cols]
        r.d_bup[:, cols] += fold8(d_pre)
        r.d_pre[at, cols] = d_pre.astype(BF16)


def consume_dattn(r, at):
    r.d_attn[at, :] = dot_nt(r.h_vm[at, :], r.w_out[...]).astype(BF16)


def spec(text):
    return P(*[name if name in ("dp", "tp") else None for name in text.split()])


def stack_all(groups):
    return [jnp.stack(group) for group in groups]


def solution(mesh):
    def device_step(x_loc, dy_loc, ln_par, bias_d, w_qkv, w_out, w_up, b_up, w_down):
        (x_in,), (dy,) = x_loc, dy_loc
        rows, width = x_in.shape
        seq = rows * mesh.shape['tp']
        n_heads, head_dim = w_qkv.shape[-2:]
        ff = w_up.shape[-1]
        lanes = n_heads * LANES

        def pad_heads(w):
            flat = w.reshape((-1, head_dim, width))
            return jnp.concatenate([flat, jnp.zeros((flat.shape[0], LANES - head_dim, width), BF16)], axis=1).reshape((-1, width))

        wqkv_t = [pad_heads(jnp.moveaxis(w, 0, -1)) for w in w_qkv]
        wo = [pad_heads(w) for w in w_out]
        parts = [w.reshape((-1, lanes, width)) for w in wqkv_t]
        (up_a, up_b), (down_a, down_b), (wq_a, wq_b), (wo_a, wo_b) = w_up, w_down, wqkv_t, wo
        bup_a, bup_b = jnp.split(b_up, 2)
        (gain_a, shift_a, gain_b, shift_b), (gain_c, shift_c, gain_d, shift_d) = ln_par
        (bias_a, bias_b), (bias_c, bias_d2) = bias_d
        part_a, part_b = [list(w) for w in parts]

        f32_rows = ((rows, width), F32)
        bf_rows = ((rows, width), BF16)
        sums = ((8, width), F32)
        keep = dict(res_out=f32_rows)
        back = dict(d_out=f32_rows, sums=sums)
        qkv_out = dict(qkv=(len(wq_a), BF16))
        dattn_out = dict(d_attn=(lanes, BF16))
        bup_acc = dict(d_bup=((8, ff), F32))
        enter, middle, leave = local_forward(rows, False, True), local_forward(rows, True, True), local_forward(rows, True, False)
        backward = local_backward(rows, False)

        u0 = unit(0, "ag_qkv0", seq, width, local=enter, local_in=dict(res=x_in, ln=jnp.stack([gain_a, shift_a])),
                  consume=consume_qkv, cons_in=dict(wqkv=wq_a), cons_out=qkv_out)
        qkv_a = u0["qkv_h"]
        dy_dep, _ = lax.optimization_barrier((dy, qkv_a))
        dy_all = lax.all_gather(dy_dep, 'tp', axis=0, tiled=True)

        attn_a, lse_a = attention_forward(qkv_a, head_dim, n_heads)
        u1 = unit(1, "out_up0", seq, width, lhs=[attn_a], weight=[wo_a], local=middle, tail=keep,
                  local_in=dict(res=x_in, ln=jnp.stack([gain_b, shift_b, bias_a])), consume=consume_up,
                  cons_in=dict(w_up=up_a, b_up=bup_a), cons_out=dict(act=(ff, BF16), gel=(ff, F32)))
        u2 = unit(2, "down_qkv1", seq, width, lhs=[u1["act_h"]], weight=[down_a], local=middle, tail=keep,
                  local_in=dict(res=u1["res_out"], ln=jnp.stack([gain_c, shift_c, bias_b])), consume=consume_qkv,
                  cons_in=dict(wqkv=wq_b), cons_out=qkv_out)
        qkv_b = u2["qkv_h"]
        attn_b, lse_b = attention_forward(qkv_b, head_dim, n_heads)
        u3 = unit(3, "out_mlp1", seq, width, lhs=[attn_b], weight=[wo_b], local=middle, tail=keep,
                  local_in=dict(res=u2["res_out"], ln=jnp.stack([gain_d, shift_d, bias_c])), consume=consume_up_down,
                  cons_in=dict(w_up=up_b, b_up=bup_b, dy=dy_all, w_down=down_b), cons_out=dict(act=(ff, BF16), d_pre=(ff, BF16)),
                  cons_acc=bup_acc)
        u4 = unit(4, "down_y", seq, width, lhs=[u3["act_h"]], weight=[down_b], local=leave, tail=dict(res_out=bf_rows),
                  local_in=dict(res=u3["res_out"], ln=jnp.stack([gain_d, shift_d, bias_d2])))

        u5 = unit(5, "dup_dattn1", seq, width, lhs=[u3["d_pre_h"]], weight=[up_b], weight_t=True, local=backward, tail=back,
                  local_in=dict(res=u3["res_out"], d_res=dy, ln=gain_d[None]), consume=consume_dattn,
                  cons_in=dict(w_out=wo_b), cons_out=dattn_out)
        dqkv_b = attention_backward(qkv_b, attn_b, u5["d_attn_h"], lse_b, head_dim, n_heads)
        u6 = unit(6, "dqkv_dpre0", seq, width, lhs=list(dqkv_b), weight=part_b, local=backward, tail=back,
                  local_in=dict(res=u2["res_out"], d_res=u5["d_out"], ln=gain_c[None]), consume=consume_dpre,
                  cons_in=dict(w_down=down_a, gel=u1["gel_h"]), cons_out=dict(d_pre=(ff, BF16)), cons_acc=bup_acc)
        u7 = unit(7, "dup_dattn0", seq, width, lhs=[u6["d_pre_h"]], weight=[up_a], weight_t=True, local=backward, tail=back,
                  local_in=dict(res=u1["res_out"], d_res=u6["d_out"], ln=gain_b[None]), consume=consume_dattn,
                  cons_in=dict(w_out=wo_a), cons_out=dattn_out)
        dqkv_a = attention_backward(qkv_a, attn_a, u7["d_attn_h"], lse_a, head_dim, n_heads)
        u7_sums, u6_sums, u5_sums = [u["sums"][:3] for u in (u7, u6, u5)]
        pair = jnp.zeros((2, width), F32)
        small = jnp.concatenate([pair, u7_sums, u6_sums, u5_sums, jnp.sum(dy.astype(F32), axis=0, keepdims=True), pair, pair])
        u8 = unit(8, "dqkv_dx", seq, width, lhs=list(dqkv_a), weight=part_a, local=local_backward(rows, True),
                  local_in=dict(res=x_in, d_res=u7["d_out"], ln=gain_a[None], small=small),
                  tail=dict(d_out=bf_rows, small_out=((16, width), F32)))
        g0, s0, g1, s1, b0, g2, s2, b1, g3, s3, b2, b3 = u8["small_out"][:12]
        ln_grad = jnp.stack(stack_all([[g0, s0, g1, s1], [g2, s2, g3, s3]]))
        bias_grad = jnp.stack(stack_all([[b0, b1], [b2, b3]]))

        def grads(lefts, rights):
            return [dot_tn(a, b).astype(BF16) for a, b in zip(lefts, rights)]

        def drop_pad(g):
            return g.reshape((-1, LANES, width))[:, :head_dim]

        g_down = grads([u1["act_h"], u3["act_h"]], [u6["h_all"], dy_all])
        g_up = grads([u1["h_all"], u3["h_all"]], [u6["d_pre_h"], u3["d_pre_h"]])
        g_out = [drop_pad(g) for g in grads([attn_a, attn_b], [u7["h_all"], u5["h_all"]])]
        g_qkv = [jnp.stack([drop_pad(g) for g in grads(d, [h] * len(d))])
                 for d, h in ((dqkv_a, u0["h_all"]), (dqkv_b, u2["h_all"]))]
        d_bup = [jnp.sum(u["d_bup"], axis=0) for u in (u6, u3)]
        g_qkv, g_out, g_up, d_bup, g_down = stack_all([g_qkv, g_out, g_up, d_bup, g_down])
        return (u4["res_out"][None], u8["d_out"][None], ln_grad, bias_grad, jnp.moveaxis(g_qkv, -1, 1), g_out, g_up, d_bup, g_down)

    tokens, rep = spec("dp tp ."), spec(". . .")
    in_specs = (tokens, tokens, rep, rep, spec(". . . tp ."), spec(". tp . ."), spec(". . tp"), spec(". tp"), spec(". tp ."))
    out_specs = (tokens, tokens, spec("dp . ."), spec("dp . ."), spec("dp . . tp ."), spec("dp tp . ."), spec("dp . tp"),
                 spec("dp tp"), spec("dp tp ."))
    return jax.shard_map(device_step, mesh=mesh, in_specs=in_specs, out_specs=out_specs, check_vma=False)
```

time: 1450 us -> 780 us (0.54)
  Pallas kernels: 0 us -> 629 us
  waiting for transfers between devices: 544 us -> 0.02 us
  matrix products: 465 us -> 69.3 us
  blocking collectives: 292 us -> 0 us
  other arithmetic: 92.9 us -> 14.6 us
  local copies, waits for them, and re-layouts: 17.5 us -> 42.4 us
  starting transfers between devices: 14.7 us -> 0.04 us
    pallas_call x0 -> x13, Pallas kernels: none -> 629 us  [the longest x9 560 us: comm_call(): pl.pallas_call(kernel, in_specs=in_specs, out_specs=[any_spec if outs[key...]
    dot_general x34 -> x12, matrix products: 379 us -> 69.3 us  [dot_tn(): lax.dot_general(a, b, (((0,), (0,)), ((), ())), preferred_element_type=F32)]
    all_to_all x4 -> x0, blocking collectives: 292 us -> none  [scatter_rows(): received = lax.all_to_all(sent, 'tp', 1, 1, tiled=True)]
    all_gather x8 -> x1, waiting for transfers between devices: 260 us -> 0.01 us  [device_step(): dy_all = lax.all_gather(dy_dep, 'tp', axis=0, tiled=True)]
    all_to_all x4 -> x0, waiting for transfers between devices: 245 us -> none  [scatter_rows(): received = lax.all_to_all(sent, 'tp', 1, 1, tiled=True)]
    unnamed x12 -> x0, matrix products: 45.6 us -> none
    sub x2 -> x0, matrix products: 39.8 us -> none  [causal_attention(): prob_bf = jax.nn.softmax(scores, axis=-1).astype(jnp.bfloat16)]
    psum x1 -> x0, waiting for transfers between devices: 38.9 us -> none  [device_step(): lax.psum((jnp.stack([grad_set[0] for grad_set in layer_grads]), jnp.stack...]
  transfers between devices with their start and end apart: 13 -> 1, of which waited for: 12 -> 0; matrix products, arithmetic and copies ran while one was open for 7% -> 2% of each run, Pallas kernels for 0% -> 23%
where the time goes in v1:
time: 780 us; the launch traced here: 771 us
  Pallas kernels  629 us (81%)
  matrix products  69.3 us (9%)
  local copies, waits for them, and re-layouts  42.4 us (5%)
  between operations  15.3 us (2%)
  other arithmetic  14.6 us (2%)
    pallas_call x9, Pallas kernels, comm_call(): pl.pallas_call(kernel, in_specs=in_specs, out_specs=[any_spec if outs[key...  560 us
    dot_general x12, matrix products, dot_tn(): lax.dot_general(a, b, (((0,), (0,)), ((), ())), preferred_element_type=F32)  69.3 us
    pallas_call x2, Pallas kernels, attention_backward(): pl.pallas_call(functools.partial(attn_bwd_kernel, head_dim ** (-0.5), n_q...  37.1 us
    pallas_call x2, Pallas kernels, attention_forward(): pl.pallas_call(functools.partial(attn_fwd_kernel, head_dim ** (-0.5), n_q...  32.7 us
  transfers between devices with their start and end apart: 1, of which 0 were waited for; matrix products, arithmetic and copies ran while one was open for 2% of the time, Pallas kernels for 23%

profile of v1, /device:TPU:0, one launch (start us, length us, event | category | flops | bytes accessed | tf_op | source)
XLA Modules:
  0.0 770.9 jit_solution(2649975540844575544)
XLA Ops:
  7.2 1.0 slice_bitcast_fusion.19
  8.2 3.5 fusion.4
  12.5 1.6 concatenate.18
  14.1 37.7 %ag_qkv0.1 = (bf16[2048,1536]{1,0:T(8,128)(2,1)}, bf16[2048,768]{1,0:T(8,128)(2,1)}) custom-call(bf16[768,1536]{1,0:T(8,128)(2,1)} %bitcast.156, bf16[256,1536]{1,0:T(8,128)(2,1)} %bitcast.169, f32[2,1536]{1,0:T(2,128)} %pad_maximum_fusion.10.refs_2_), custom_call_target="tpu_custom_call" | custom-call | flops 4831938048 | bytes 30000000 | tf_op jit(solution)/shard_map/ag_qkv0/pallas_call | solution.py:414
  52.0 1.4 slice_bitcast_fusion.12
  53.4 0.9 concatenate.21
  55.3 1.7 concatenate.20
  57.0 16.3 %attn_fwd.2 = (bf16[2048,256]{1,0:T(8,128)(2,1)S(1)}, f32[2,1,2048]{2,1,0:T(1,128)S(1)}) custom-call(bf16[2048,768]{1,0:T(8,128)(2,1)S(1)} %copy-done, bf16[2048,768]{1,0:T(8,128)(2,1)S(1)} %copy-done, bf16[2048,768]{1,0:T(8,128)(2,1)S(1)} %copy-done), custom_call_target="tpu_custom_call" | custom-call | flops 2147483648 | bytes 4194304 | tf_op jit(solution)/shard_map/attn_fwd/pallas_call | solution.py:71
  74.8 2.5 slice_bitcast_fusion.1
  77.6 2.5 slice_bitcast_fusion
  80.1 71.9 %out_up0.1 = (f32[256,1536]{1,0:T(8,128)}, bf16[2048,1536]{1,0:T(8,128)(2,1)}, bf16[2048,768]{1,0:T(8,128)(2,1)}, f32[2048,768]{1,0:T(8,128)}) custom-call(bf16[2048,256]{1,0:T(8,128)(2,1)} %copy-done.3, bf16[256,1536]{1,0:T(8,128)(2,1)} %bitcast.157, bf16[1536,768]{1,0:T(8,128)(2,1)} %get-tuple-element.92.refs_2_.refs_1_, ...), custom_call_target="tpu_custom_call" | custom-call | flops 11274389504 | bytes 30000000 | tf_op jit(solution)/shard_map/out_up0/pallas_call | solution.py:414
  152.0 71.7 %down_qkv1.1 = (f32[256,1536]{1,0:T(8,128)}, bf16[2048,1536]{1,0:T(8,128)(2,1)}, bf16[2048,768]{1,0:T(8,128)(2,1)}) custom-call(bf16[2048,768]{1,0:T(8,128)(2,1)} %get-tuple-element.51.refs_0_, bf16[768,1536]{1,0:T(8,128)(2,1)} %get-tuple-element.90.refs_1_.refs_6_, bf16[768,1536]{1,0:T(8,128)(2,1)} %bitcast.155, f32[256,1536]{1,0:T(8,128)} %get-tuple-element.52.refs_3_, ...), custom_call_target="tpu_custom_call" | custom-call | flops 9663776768 | bytes 30000000 | tf_op jit(solution)/shard_map/down_qkv1/pallas_call | solution.py:414
  223.7 1.9 copy-done.1
  225.6 16.3 %attn_fwd.3 = (bf16[2048,256]{1,0:T(8,128)(2,1)S(1)}, f32[2,1,2048]{2,1,0:T(1,128)S(1)}) custom-call(bf16[2048,768]{1,0:T(8,128)(2,1)S(1)} %copy-done.1, bf16[2048,768]{1,0:T(8,128)(2,1)S(1)} %copy-done.1, bf16[2048,768]{1,0:T(8,128)(2,1)S(1)} %copy-done.1), custom_call_target="tpu_custom_call" | custom-call | flops 2147483648 | bytes 4194304 | tf_op jit(solution)/shard_map/attn_fwd/pallas_call | solution.py:71
  242.0 1.0 copy-done.6
  243.6 1.4 pad_slice_fusion.3
  245.1 1.5 pad_slice_fusion
  246.5 69.1 %out_mlp1.1 = (f32[256,1536]{1,0:T(8,128)}, bf16[2048,1536]{1,0:T(8,128)(2,1)}, bf16[2048,768]{1,0:T(8,128)(2,1)}, bf16[2048,768]{1,0:T(8,128)(2,1)}, f32[8,768]{1,0:T(8,128)}) custom-call(bf16[2048,256]{1,0:T(8,128)(2,1)} %copy-done.6, bf16[256,1536]{1,0:T(8,128)(2,1)} %bitcast.161, bf16[1536,768]{1,0:T(8,128)(2,1)} %get-tuple-element.91.refs_2_.refs_1_, ...), custom_call_target="tpu_custom_call" | custom-call | flops 11274389504 | bytes 30000000 | tf_op jit(solution)/shard_map/out_mlp1/pallas_call | solution.py:414
  315.7 72.5 %dup_dattn1.1 = (f32[256,1536]{1,0:T(8,128)}, f32[8,1536]{1,0:T(8,128)}, bf16[2048,1536]{1,0:T(8,128)(2,1)}, bf16[2048,256]{1,0:T(8,128)(2,1)}) custom-call(bf16[2048,768]{1,0:T(8,128)(2,1)} %get-tuple-element.59.refs_0_, bf16[1536,768]{1,0:T(8,128)(2,1)} %get-tuple-element.91.refs_2_.refs_1_, bf16[256,1536]{1,0:T(8,128)(2,1)} %bitcast.162, ...), custom_call_target="tpu_custom_call" | custom-call | flops 6442550784 | bytes 30000000 | tf_op jit(solution)/shard_map/dup_dattn1/pallas_call | solution.py:414
  388.2 1.9 copy-done.2
  390.1 1.2 copy-done.7
  391.3 1.2 copy-done.16
  392.6 18.6 %attn_bwd.2 = (bf16[2048,256]{1,0:T(8,128)(2,1)S(1)}, bf16[2048,256]{1,0:T(8,128)(2,1)S(1)}, bf16[2048,256]{1,0:T(8,128)(2,1)S(1)}) custom-call(bf16[2048,768]{1,0:T(8,128)(2,1)S(1)} %copy-done.2, bf16[2048,768]{1,0:T(8,128)(2,1)S(1)} %copy-done.2, bf16[2048,768]{1,0:T(8,128)(2,1)S(1)} %copy-done.2, bf16[2048,256]{1,0:T(8,128)(2,1)S(1)} %copy-done.7, ...), custom_call_target="tpu_custom_call" | custom-call | flops 5368709120 | bytes 8388608 | tf_op jit(solution)/shard_map/attn_bwd/pallas_call | solution.py:134
  411.2 6.6 convolution_convert_fusion.6
  417.8 5.6 convolution_convert_fusion.7
  423.5 2.7 convolution_convert_fusion.8
  426.2 73.8 %dqkv_dpre0.1 = (f32[256,1536]{1,0:T(8,128)}, f32[8,1536]{1,0:T(8,128)}, bf16[2048,1536]{1,0:T(8,128)(2,1)}, bf16[2048,768]{1,0:T(8,128)(2,1)}, f32[8,768]{1,0:T(8,128)}) custom-call(bf16[2048,256]{1,0:T(8,128)(2,1)} %copy-done.12, bf16[256,1536]{1,0:T(8,128)(2,1)} %bitcast.167, bf16[2048,256]{1,0:T(8,128)(2,1)} %copy-done.13, bf16[256,1536]{1,0:T(8,128)(2,1)} %bitcast.168, ...), custom_call_target="tpu_custom_call" | custom-call | flops 9663776768 | bytes 30000000 | tf_op jit(solution)/shard_map/dqkv_dpre0/pallas_call | solution.py:414
  500.1 73.5 %dup_dattn0.1 = (f32[256,1536]{1,0:T(8,128)}, f32[8,1536]{1,0:T(8,128)}, bf16[2048,1536]{1,0:T(8,128)(2,1)}, bf16[2048,256]{1,0:T(8,128)(2,1)}) custom-call(bf16[2048,768]{1,0:T(8,128)(2,1)} %get-tuple-element.67.refs_0_, bf16[1536,768]{1,0:T(8,128)(2,1)} %get-tuple-element.92.refs_2_.refs_1_, bf16[256,1536]{1,0:T(8,128)(2,1)} %bitcast.158, ...), custom_call_target="tpu_custom_call" | custom-call | flops 6442550784 | bytes 30000000 | tf_op jit(solution)/shard_map/dup_dattn0/pallas_call | solution.py:414
  574.5 1.2 copy-done.4
  575.7 1.2 copy-done.15
  576.9 18.6 %attn_bwd.3 = (bf16[2048,256]{1,0:T(8,128)(2,1)S(1)}, bf16[2048,256]{1,0:T(8,128)(2,1)S(1)}, bf16[2048,256]{1,0:T(8,128)(2,1)S(1)}) custom-call(bf16[2048,768]{1,0:T(8,128)(2,1)S(1)} %copy-done, bf16[2048,768]{1,0:T(8,128)(2,1)S(1)} %copy-done, bf16[2048,768]{1,0:T(8,128)(2,1)S(1)} %copy-done, bf16[2048,256]{1,0:T(8,128)(2,1)S(1)} %copy-done.4, ...), custom_call_target="tpu_custom_call" | custom-call | flops 5368709120 | bytes 8388608 | tf_op jit(solution)/shard_map/attn_bwd/pallas_call | solution.py:134
  595.5 5.7 convolution_convert_fusion.9
  601.3 5.6 convolution_convert_fusion.10
  606.9 2.7 convolution_convert_fusion.11
  609.7 1.3 concatenate.23.refs_9_
  611.0 51.9 %dqkv_dx.1 = (bf16[256,1536]{1,0:T(8,128)(2,1)}, f32[16,1536]{1,0:T(8,128)}) custom-call(bf16[2048,256]{1,0:T(8,128)(2,1)} %copy-done.9, bf16[256,1536]{1,0:T(8,128)(2,1)} %bitcast.164, bf16[2048,256]{1,0:T(8,128)(2,1)} %copy-done.10, bf16[256,1536]{1,0:T(8,128)(2,1)} %bitcast.165, bf16[2048,256]{1,0:T(8,128)(2,1)} %copy-done.11, ...), custom_call_target="tpu_custom_call" | custom-call | flops 4831938048 | bytes 30000000 | tf_op jit(solution)/shard_map/dqkv_dx/pallas_call | solution.py:414
  665.4 37.3 %down_y.1 = bf16[256,1536]{1,0:T(8,128)(2,1)} custom-call(bf16[2048,768]{1,0:T(8,128)(2,1)} %get-tuple-element.57.refs_0_, bf16[768,1536]{1,0:T(8,128)(2,1)} %get-tuple-element.89.refs_5_.refs_1_, f32[256,1536]{1,0:T(8,128)} %get-tuple-element.58.refs_2_.refs_3_, f32[3,1536]{1,0:T(4,128)} %get-tuple-element.120.refs_3_), custom_call_target="tpu_custom_call" | custom-call | flops 4831938048 | bytes 30000000 | tf_op jit(solution)/shard_map/down_y/pallas_call | solution.py:414
  702.7 9.3 %fusion.1 = bf16[1,1536,768]{2,1,0:T(8,128)(2,1)} fusion(bf16[2048,1536]{1,0:T(8,128)(2,1)} %get-tuple-element.85, bf16[2048,768]{1,0:T(8,128)(2,1)} %get-tuple-element.59.refs_0_), kind=kOutput, calls=%fused_computation.8 | convolution fusion | flops 4833017856 | bytes 11796480 | tf_op jit(solution)/shard_map/dot_general | solution.py:28
  712.1 4.7 convolution_convert_fusion.4
  716.9 9.4 %fusion = bf16[1,1536,768]{2,1,0:T(8,128)(2,1)} fusion(bf16[2048,1536]{1,0:T(8,128)(2,1)} %get-tuple-element.84, bf16[2048,768]{1,0:T(8,128)(2,1)S(1)} %copy-done.46), kind=kOutput, calls=%fused_computation.7 | convolution fusion | flops 4833017856 | bytes 11796480 | tf_op jit(solution)/shard_map/dot_general | solution.py:28
  728.9 6.8 fusion.2
  735.7 1.8 convolution_convert_fusion.5
  739.5 1.5 copy-done.32
  740.9 4.4 pad_maximum_fusion
  745.4 8.2 %fusion.3 = bf16[1,768,1536]{2,1,0:T(8,128)(2,1)S(1)} fusion(bf16[2048,768]{1,0:T(8,128)(2,1)S(1)} %copy-done.48, bf16[2048,1536]{1,0:T(8,128)(2,1)} %all-gather.2.cloned.1.call-done.refs_4_), kind=kOutput, calls=%fused_computation.10 | convolution fusion | flops 4833017856 | bytes 11796480 | tf_op jit(solution)/shard_map/dot_general | solution.py:28
  753.7 2.6 pad_maximum_fusion.1
  756.3 1.1 pad_maximum_fusion.2
  758.5 2.1 maximum_bitcast_fusion
  (160 shorter events, 16.3 us)
Async XLA Ops:
  7.2 239.4 %all-gather.2.cloned.1.call-start = ((), (), s32[]{:S(2)}) async-start(), calls=%async_computation | async-start | bytes 7077888 | tf_op jit(solution)/shard_map/all_gather | solution.py:696
  8.2 3.6 copy-start.40
  8.2 65.8 %copy-start.41 = (f32[1,1536]{1,0:T(1,128)}, f32[1,1536]{1,0:T(1,128)S(1)}, u32[]{:S(2)}) copy-start(f32[1,1536]{1,0:T(1,128)S(1)} %get-tuple-element.112.refs_5_) | copy-start | bytes 18436
  8.2 65.8 %copy-start.42 = (f32[1,1536]{1,0:T(1,128)}, f32[1,1536]{1,0:T(1,128)S(1)}, u32[]{:S(2)}) copy-start(f32[1,1536]{1,0:T(1,128)S(1)} %get-tuple-element.110.refs_10_) | copy-start | bytes 18436
  8.2 234.7 %copy-start.36 = (f32[1,1536]{1,0:T(1,128)}, f32[1,1536]{1,0:T(1,128)S(1)}, u32[]{:S(2)}) copy-start(f32[1,1536]{1,0:T(1,128)S(1)} %get-tuple-element.108.refs_5_) | copy-start | bytes 18436
  11.8 40.0 %copy-start.19 = (bf16[1,1536,3,2,96]{1,4,3,2,0:T(8,128)(2,1)}, bf16[1,1536,3,2,96]{1,4,3,2,0:T(8,128)(2,1)S(1)}, u32[]{:S(2)}) copy-start(bf16[1,1536,3,2,96]{1,4,3,2,0:T(8,128)(2,1)S(1)} %get-tuple-element.94) | copy-start | bytes 5308420
  14.1 37.8 %copy-start.21 = (bf16[1,256,1536]{2,1,0:T(8,128)(2,1)S(1)}, bf16[1,256,1536]{2,1,0:T(8,128)(2,1)}, u32[]{:S(2)}) copy-start(bf16[1,256,1536]{2,1,0:T(8,128)(2,1)} %param.10) | copy-start | bytes 2359300
  51.9 3.5 copy-start.17
  53.4 3.5 copy-start
  55.3 19.4 %slice-start.6 = ((s8[4718592]{0:T(1024)(128)(4,1)}), s8[4194304]{0:T(1024)(128)(4,1)S(1)}, s32[]{:S(2)}) async-start(s8[4718592]{0:T(1024)(128)(4,1)} %bitcast.141), calls=%async_computation.7 | async-start | bytes 8388608
  57.0 16.4 %copy-start.45 = (f32[2,768]{1,0:T(2,128)S(1)}, f32[2,768]{1,0:T(2,128)}, u32[]{:S(2)}) copy-start(f32[2,768]{1,0:T(2,128)} %param.16) | copy-start | bytes 18436
  57.0 17.0 %copy-start.37 = (f32[2,2,1536]{2,1,0:T(2,128)S(1)}, f32[2,2,1536]{2,1,0:T(2,128)}, u32[]{:S(2)}) copy-start(f32[2,2,1536]{2,1,0:T(2,128)} %param.12) | copy-start | bytes 73732
  57.0 17.8 %slice-start.7 = ((s8[4718592]{0:T(1024)(128)(4,1)}), s8[524288]{0:T(1024)(128)(4,1)S(1)}, s32[]{:S(2)}) async-start(s8[4718592]{0:T(1024)(128)(4,1)} %bitcast.141), calls=%async_computation.8 | async-start | bytes 1048576
  73.4 3.9 copy-start.3
  74.1 3.2 slice-start.8
  225.6 18.0 %copy-start.20 = (bf16[1,1536,3,2,96]{1,4,3,2,0:T(8,128)(2,1)S(1)}, bf16[1,1536,3,2,96]{1,4,3,2,0:T(8,128)(2,1)}, u32[]{:S(2)}) copy-start(bf16[1,1536,3,2,96]{1,4,3,2,0:T(8,128)(2,1)} %copy-done.19) | copy-start | bytes 5308420
  411.1 6.7 copy-start.14
  411.2 6.7 copy-start.13
  411.2 12.3 %copy-start.12 = (bf16[2048,256]{1,0:T(8,128)(2,1)}, bf16[2048,256]{1,0:T(8,128)(2,1)S(1)}, u32[]{:S(2)}) copy-start(bf16[2048,256]{1,0:T(8,128)(2,1)S(1)} %get-tuple-element.62.refs_0_) | copy-start | bytes 3145732
  411.2 12.3 %slice-start.2 = ((s8[6291456]{0:T(1024)(128)(4,1)}), s8[4194304]{0:T(1024)(128)(4,1)S(1)}, s32[]{:S(2)}) async-start(s8[6291456]{0:T(1024)(128)(4,1)} %bitcast.133), calls=%async_computation.3 | async-start | bytes 8388608
  417.8 5.6 slice-start.3
  500.0 74.4 %copy-start.44 = (f32[8,1536]{1,0:T(8,128)S(1)}, f32[8,1536]{1,0:T(8,128)}, u32[]{:S(2)}) copy-start(f32[8,1536]{1,0:T(8,128)} %get-tuple-element.76) | copy-start | bytes 147460
  500.1 74.4 %copy-start.43 = (f32[8,1536]{1,0:T(8,128)S(1)}, f32[8,1536]{1,0:T(8,128)}, u32[]{:S(2)}) copy-start(f32[8,1536]{1,0:T(8,128)} %get-tuple-element.77) | copy-start | bytes 147460
  595.5 5.8 copy-start.11
  595.5 5.8 copy-start.10
  595.5 11.4 %copy-start.9 = (bf16[2048,256]{1,0:T(8,128)(2,1)}, bf16[2048,256]{1,0:T(8,128)(2,1)S(1)}, u32[]{:S(2)}) copy-start(bf16[2048,256]{1,0:T(8,128)(2,1)S(1)} %get-tuple-element.71.refs_0_) | copy-start | bytes 3145732
  595.5 11.4 %slice-start = ((s8[6291456]{0:T(1024)(128)(4,1)}), s8[4194304]{0:T(1024)(128)(4,1)S(1)}, s32[]{:S(2)}) async-start(s8[6291456]{0:T(1024)(128)(4,1)} %bitcast.131), calls=%async_computation.1 | async-start | bytes 8388608
  601.3 5.6 slice-start.1
  702.7 9.3 %copy-start.38 = (f32[8,768]{1,0:T(8,128)S(1)}, f32[8,768]{1,0:T(8,128)}, u32[]{:S(2)}) copy-start(f32[8,768]{1,0:T(8,128)} %get-tuple-element.87) | copy-start | bytes 73732
  702.7 9.3 %copy-start.8 = (bf16[2048,256]{1,0:T(8,128)(2,1)S(1)}, bf16[2048,256]{1,0:T(8,128)(2,1)}, u32[]{:S(2)}) copy-start(bf16[2048,256]{1,0:T(8,128)(2,1)} %copy-done.6) | copy-start | bytes 3145732
  712.1 4.8 copy-start.46
  712.1 16.8 %slice-start.10 = ((s8[6291456]{0:T(1024)(128)(4,1)}), s8[4194304]{0:T(1024)(128)(4,1)S(1)}, s32[]{:S(2)}) async-start(s8[6291456]{0:T(1024)(128)(4,1)} %bitcast.172), calls=%async_computation.11 | async-start | bytes 8388608
  716.8 9.4 %copy-start.24 = (bf16[256,1536]{1,0:T(8,128)(2,1)S(1)}, bf16[256,1536]{1,0:T(8,128)(2,1)}, u32[]{:S(2)}) copy-start(bf16[256,1536]{1,0:T(8,128)(2,1)} %convolution_convert_fusion.8) | copy-start | bytes 2359300
  716.9 10.3 %copy-start.23 = (bf16[256,1536]{1,0:T(8,128)(2,1)S(1)}, bf16[256,1536]{1,0:T(8,128)(2,1)}, u32[]{:S(2)}) copy-start(bf16[256,1536]{1,0:T(8,128)(2,1)} %convolution_convert_fusion.7) | copy-start | bytes 2359300
  716.9 11.2 %copy-start.22 = (bf16[256,1536]{1,0:T(8,128)(2,1)S(1)}, bf16[256,1536]{1,0:T(8,128)(2,1)}, u32[]{:S(2)}) copy-start(bf16[256,1536]{1,0:T(8,128)(2,1)} %convolution_convert_fusion.6) | copy-start | bytes 2359300
  716.9 12.0 %slice-start.11 = ((s8[6291456]{0:T(1024)(128)(4,1)}), s8[2097152]{0:T(1024)(128)(4,1)S(1)}, s32[]{:S(2)}) async-start(s8[6291456]{0:T(1024)(128)(4,1)} %bitcast.172), calls=%async_computation.12 | async-start | bytes 4194304
  727.1 8.5 %slice-start.4 = ((s8[6291456]{0:T(1024)(128)(4,1)}), s8[4194304]{0:T(1024)(128)(4,1)S(1)}, s32[]{:S(2)}) async-start(s8[6291456]{0:T(1024)(128)(4,1)} %bitcast.135), calls=%async_computation.5 | async-start | bytes 8388608
  728.9 6.8 copy-start.5
  728.9 6.8 slice-start.5
  735.7 3.6 copy-start.39
  735.7 3.6 copy-start.26
  740.9 4.4 copy-start.48
  745.4 8.3 %copy-start.33 = (bf16[1,768,1536]{2,1,0:T(8,128)(2,1)S(1)}, bf16[1,768,1536]{2,1,0:T(8,128)(2,1)}, u32[]{:S(2)}) copy-start(bf16[1,768,1536]{2,1,0:T(8,128)(2,1)} %fusion.2) | copy-start | bytes 7077892
  753.7 4.4 copy-start.27
  753.7 4.3 copy-start.28
  753.7 4.3 copy-start.29
  758.4 3.4 copy-start.35
  758.4 4.3 copy-start.34
  (14 other events, 26.1 us)
Sparse Core Ops, SparseCore 0:
  52.0 43.5 all-gather.1

commit v2 on v1

v2 whole, which is shorter than its diff:
```python
import functools
import math

import jax
import jax.numpy as jnp
from jax import lax
from jax.experimental import pallas as pl
from jax.experimental.pallas import tpu as pltpu
from jax.sharding import PartitionSpec as P

MESH = pl.DeviceIdType.MESH
BF16 = jnp.bfloat16
F32 = jnp.float32
LOG2E = math.log2(math.e)
VMEM_LIMIT = 60 * 1024 * 1024
LANES = 128


def dot_nn(a, b):
    return lax.dot_general(a, b, (((1,), (0,)), ((), ())), preferred_element_type=F32)


def dot_nt(a, b):
    return lax.dot_general(a, b, (((1,), (1,)), ((), ())), preferred_element_type=F32)


def dot_tn(a, b):
    return lax.dot_general(a, b, (((0,), (0,)), ((), ())), preferred_element_type=F32)


def attn_fwd_kernel(scale, n_q, q_ref, k_ref, v_ref, a_ref, lse_ref):
    blk = q_ref.shape[0]
    coef = scale * LOG2E
    row = lax.broadcasted_iota(jnp.int32, (blk, blk), 0)
    col = lax.broadcasted_iota(jnp.int32, (blk, blk), 1)

    def variant(i):
        q = q_ref[...]
        parts = []
        for j in range(i + 1):
            s = dot_nt(q, k_ref[j * blk:(j + 1) * blk, :])
            if j == i:
                s = jnp.where(row >= col, s, -1e30)
            parts.append(s)
        top = parts[0]
        for s in parts[1:]:
            top = jnp.maximum(top, s)
        top = jnp.max(top, axis=-1, keepdims=True) * coef
        parts = [jnp.exp2(s * coef - top) for s in parts]
        total = parts[0]
        for e in parts[1:]:
            total = total + e
        total = jnp.sum(total, axis=-1, keepdims=True)
        inv = 1.0 / total
        out = None
        for j, e in enumerate(parts):
            o = dot_nn((e * inv).astype(BF16), v_ref[j * blk:(j + 1) * blk, :])
            out = o if out is None else out + o
        a_ref[...] = out.astype(BF16)
        lse = jnp.broadcast_to(top + jnp.log2(total), (blk, 128))
        lse_ref[0] = jnp.transpose(lse)[0:1, :]

    for i in range(n_q):
        pl.when(pl.program_id(1) == i)(functools.partial(variant, i))


def attention_forward(qkv, head_dim, n_heads):
    seq = qkv.shape[0]
    blk = 512
    n_q = seq // blk
    return pl.pallas_call(
        functools.partial(attn_fwd_kernel, head_dim ** -0.5, n_q),
        grid=(n_heads, n_q),
        in_specs=[pl.BlockSpec((blk, 128), lambda h, i: (i, h)),
                  pl.BlockSpec((seq, 128), lambda h, i: (0, n_heads + h)),
                  pl.BlockSpec((seq, 128), lambda h, i: (0, 2 * n_heads + h))],
        out_specs=[pl.BlockSpec((blk, 128), lambda h, i: (i, h)),
                   pl.BlockSpec((1, 1, blk), lambda h, i: (h, 0, i))],
        out_shape=[jax.ShapeDtypeStruct((seq, n_heads * 128), BF16),
                   jax.ShapeDtypeStruct((n_heads, 1, seq), F32)],
        compiler_params=pltpu.CompilerParams(dimension_semantics=("arbitrary", "arbitrary"), vmem_limit_bytes=40 * 1024 * 1024),
        cost_estimate=pl.CostEstimate(flops=4 * seq * seq * 128, bytes_accessed=8 * seq * 256, transcendentals=seq * seq),
        name="attn_fwd",
    )(qkv, qkv, qkv)


def attn_bwd_kernel(scale, n_q, q_ref, k_ref, v_ref, a_ref, da_ref, lse_ref, dq_ref, dk_ref, dv_ref, dk_acc, dv_acc):
    blk = q_ref.shape[0]
    coef = scale * LOG2E
    key = lax.broadcasted_iota(jnp.int32, (blk, blk), 0)
    qry = lax.broadcasted_iota(jnp.int32, (blk, blk), 1)

    def variant(i):
        q = q_ref[...]
        da = da_ref[...]
        lse = lse_ref[0]
        row_dot = jnp.sum(jnp.transpose(da.astype(F32) * a_ref[...].astype(F32)), axis=0, keepdims=True)
        dq = None
        for j in range(i, -1, -1):
            rows = slice(j * blk, (j + 1) * blk)
            k = k_ref[rows, :]
            p = jnp.exp2(dot_nt(k, q) * coef - lse)
            if j == i:
                p = jnp.where(qry >= key, p, 0.0)
            dv = dot_nn(p.astype(BF16), da)
            ds = (p * (dot_nt(v_ref[rows, :], da) - row_dot)).astype(BF16)
            dk = dot_nn(ds, q)
            if j == i:
                dv_acc[rows, :] = dv
                dk_acc[rows, :] = dk
            else:
                dv_acc[rows, :] += dv
                dk_acc[rows, :] += dk
            d = dot_tn(ds, k)
            dq = d if dq is None else dq + d
        dq_ref[...] = (dq * scale).astype(BF16)

    for i in range(n_q):
        pl.when(pl.program_id(1) == i)(functools.partial(variant, i))

    @pl.when(pl.program_id(1) == n_q - 1)
    def _():
        dk_ref[...] = (dk_acc[...] * scale).astype(BF16)
        dv_ref[...] = dv_acc[...].astype(BF16)


def attention_backward(qkv, attn, d_attn, lse, head_dim, n_heads):
    seq = qkv.shape[0]
    blk = 512
    n_q = seq // blk
    row = pl.BlockSpec((blk, 128), lambda h, i: (i, h))
    full = pl.BlockSpec((seq, 128), lambda h, i: (0, h))
    shape = jax.ShapeDtypeStruct((seq, n_heads * 128), BF16)
    return pl.pallas_call(
        functools.partial(attn_bwd_kernel, head_dim ** -0.5, n_q),
        grid=(n_heads, n_q),
        in_specs=[row,
                  pl.BlockSpec((seq, 128), lambda h, i: (0, n_heads + h)),
                  pl.BlockSpec((seq, 128), lambda h, i: (0, 2 * n_heads + h)),
                  row, row,
                  pl.BlockSpec((1, 1, blk), lambda h, i: (h, 0, i))],
        out_specs=[row, full, full],
        out_shape=[shape, shape, shape],
        scratch_shapes=[pltpu.VMEM((seq, 128), F32), pltpu.VMEM((seq, 128), F32)],
        compiler_params=pltpu.CompilerParams(dimension_semantics=("arbitrary", "arbitrary"), vmem_limit_bytes=40 * 1024 * 1024),
        cost_estimate=pl.CostEstimate(flops=10 * seq * seq * 128, bytes_accessed=16 * seq * 256, transcendentals=seq * seq),
        name="attn_bwd",
    )(qkv, qkv, qkv, attn, d_attn, lse)


class Place:
    def __init__(self):
        t = lax.axis_index("tp")
        self.me = t
        self.dc = 1 - 2 * (t % 2)
        self.dx = 2 - 4 * ((t // 2) % 2)
        self.dy = 4 - 8 * (t // 4)
        self.partner = t + self.dc
        self.xn = t + self.dx
        self.yn = t + self.dy


def barrier(pos):
    sem = pltpu.get_barrier_semaphore()
    for peer in (pos.partner, pos.xn, pos.yn):
        pl.semaphore_signal(sem, inc=1, device_id={"tp": peer}, device_id_type=MESH)
    pl.semaphore_wait(sem, 3)


def rdma(src, dst, sems, idx, peer):
    send, recv = sems
    return pltpu.make_async_remote_copy(src_ref=src, dst_ref=dst, send_sem=send.at[idx], recv_sem=recv.at[idx],
                                        device_id={"tp": peer}, device_id_type=MESH)


def rs_scratch(half, width):
    quarter = half // 2
    return dict(
        rs_snd=pltpu.VMEM((2, 4, half, width), BF16), rs_rcv=pltpu.VMEM((2, 4, half, width), BF16),
        rs_sum=pltpu.VMEM((2, 4, half, width), F32), rs_out=pltpu.VMEM((2, 3, half, width), BF16),
        rs_in=pltpu.VMEM((2, 6, quarter, width), BF16),
        rs_psend=pltpu.SemaphoreType.DMA((2, 4)), rs_precv=pltpu.SemaphoreType.DMA((2, 4)),
        rs_send=pltpu.SemaphoreType.DMA((2, 6)), rs_recv=pltpu.SemaphoreType.DMA((2, 6)))


class ReduceScatter:
    def __init__(self, pos, r, hf, half, width, produce, n_chunk=3):
        self.pos, self.r, self.hf, self.half, self.produce = pos, r, hf, half, produce
        self.cols = [pl.ds(c * (width // n_chunk), width // n_chunk) for c in range(n_chunk)]
        self.quarter = half // 2
        top, low = pl.ds(0, self.quarter), pl.ds(self.quarter, self.quarter)
        sems = (r.rs_send.at[hf], r.rs_recv.at[hf])

        def hop(i, slot, part, peer):
            return rdma(r.rs_out.at[hf, slot, part], r.rs_in.at[hf, i], sems, i, peer)

        self.diag_x, self.diag_y = hop(0, 0, top, pos.xn), hop(1, 0, low, pos.yn)
        self.x_top, self.x_low = hop(2, 1, top, pos.xn), hop(3, 1, low, pos.xn)
        self.y_top, self.y_low = hop(4, 2, top, pos.yn), hop(5, 2, low, pos.yn)

    def dest(self, k):
        return self.pos.me + (1 - k // 2) * self.pos.dx + (1 - k % 2) * self.pos.dy

    def to_partner(self, k):
        r, hf = self.r, self.hf
        return rdma(r.rs_snd.at[hf, k], r.rs_rcv.at[hf, k], (r.rs_psend.at[hf], r.rs_precv.at[hf]), k, self.pos.partner)

    def compute(self, send):
        r, hf = self.r, self.hf

        def first(k, carry):
            for cols in self.cols:
                r.rs_snd[hf, k, :, cols] = self.produce(self.dest(k) + self.pos.dc, cols).astype(BF16)
            self.to_partner(k).start()
            return carry

        lax.fori_loop(0, 4, first, 0)

        def second(k, carry):
            self.to_partner(k).wait_recv()
            for cols in self.cols:
                total = self.produce(self.dest(k), cols) + r.rs_rcv[hf, k, :, cols].astype(F32)
                r.rs_sum[hf, k, :, cols] = total

                @pl.when(k < 3)
                def _():
                    r.rs_out[hf, k, :, cols] = r.rs_sum[hf, k, :, cols].astype(BF16)

            if send:
                self.send(k)
            return carry

        lax.fori_loop(0, 4, second, 0)

    def send(self, k):
        @pl.when(k == 0)
        def _():
            self.diag_x.start()
            self.diag_y.start()

        @pl.when(k == 1)
        def _():
            self.x_top.start()

        @pl.when(k == 2)
        def _():
            self.y_low.start()

    def send_all(self):
        for copy in (self.diag_x, self.diag_y, self.x_top, self.y_low):
            copy.start()

    def relay(self):
        r, hf = self.r, self.hf

        def add(slot, part):
            def body(i, carry):
                rr = pl.ds(pl.multiple_of(i * 16, 16), 16)
                at = pl.ds(pl.multiple_of(part * self.quarter + i * 16, 16), 16)
                r.rs_out[hf, slot, at, :] = (r.rs_sum[hf, slot, at, :] + r.rs_in[hf, part, rr, :].astype(F32)).astype(BF16)
                return carry

            lax.fori_loop(0, self.quarter // 16, body, 0)

        self.diag_x.wait_recv()
        add(2, 0)
        self.y_top.start()
        self.diag_y.wait_recv()
        add(1, 1)
        self.x_low.start()

    def finish(self):
        for copy in (self.x_top, self.y_low, self.y_top, self.x_low):
            copy.wait_recv()

    def rows(self, start, count):
        r, hf = self.r, self.hf
        part = start // self.quarter
        inner = pl.ds(pl.multiple_of(start - part * self.quarter, count), count)
        mine = r.rs_sum[hf, 3, pl.ds(start, count), :]
        return (mine + r.rs_in[hf, 2 + part, inner, :].astype(F32)) + r.rs_in[hf, 4 + part, inner, :].astype(F32)

    def drain(self):
        for k in range(4):
            self.to_partner(k).wait_send()
        for copy in (self.diag_x, self.diag_y, self.x_top, self.x_low, self.y_top, self.y_low):
            copy.wait_send()


def ag_scratch(seq, width):
    return dict(h_vm=pltpu.VMEM((seq, width), BF16), h_out=pltpu.SemaphoreType.DMA((2, 8)),
                ag_send=pltpu.SemaphoreType.DMA((2, 13)), ag_recv=pltpu.SemaphoreType.DMA((2, 13)))


class AllGather:
    def __init__(self, pos, r, hf, half, consume, streams):
        self.pos, self.hf, self.half, self.consume, self.streams = pos, hf, half, consume, streams
        quarter = half // 2
        sems = (r.ag_send.at[hf], r.ag_recv.at[hf])
        me, xn, yn, mate = pos.me, pos.xn, pos.yn, pos.partner
        dn = me + pos.dx + pos.dy

        def copy(i, owner, part, peer):
            ref = r.h_vm.at[pl.ds(pl.multiple_of(owner * 2 * half + hf * half + part * quarter, quarter), quarter)]
            return rdma(ref, ref, sems, i, peer)

        ref = r.h_vm.at[pl.ds(pl.multiple_of(me * 2 * half + hf * half, half), half)]
        self.own_p = rdma(ref, ref, sems, 0, mate)
        self.own_xa, self.own_xb = copy(1, me, 0, xn), copy(2, me, 1, xn)
        self.own_ya, self.own_yb = copy(3, me, 0, yn), copy(4, me, 1, yn)
        self.relay_y = copy(5, xn, 0, yn)
        self.relay_x = copy(6, yn, 1, xn)
        self.fwd_xa, self.fwd_xb = copy(7, xn, 0, mate), copy(8, xn, 1, mate)
        self.fwd_ya, self.fwd_yb = copy(9, yn, 0, mate), copy(10, yn, 1, mate)
        self.fwd_da, self.fwd_db = copy(11, dn, 0, mate), copy(12, dn, 1, mate)

    def start(self):
        for copy in (self.own_xa, self.own_yb, self.own_xb, self.own_ya, self.own_p):
            copy.start()

    def relay(self):
        self.own_xa.wait_recv()
        self.relay_y.start()
        self.fwd_xa.start()
        self.own_yb.wait_recv()
        self.relay_x.start()
        self.fwd_yb.start()

    def second(self):
        self.own_xb.wait_recv()
        self.fwd_xb.start()
        self.own_ya.wait_recv()
        self.fwd_ya.start()

    def last(self):
        self.relay_y.wait_recv()
        self.fwd_da.start()
        self.relay_x.wait_recv()
        self.fwd_db.start()

    def out_copies(self, s):
        pos = self.pos
        block = pos.me + (s % 2) * pos.dc + ((s // 2) % 2) * pos.dx + (s // 4) * pos.dy
        at = pl.ds(pl.multiple_of(block * 2 * self.half + self.hf * self.half, self.half), self.half)
        return at, [pltpu.make_async_copy(src.at[at], dst.at[at], sem.at[self.hf, s]) for src, dst, sem in self.streams]

    def use(self, first, until):
        def step(s, carry):
            @pl.when(s == 1)
            def _():
                self.own_p.wait_recv()

            @pl.when(s == 3)
            def _():
                self.fwd_xa.wait_recv()
                self.fwd_xb.wait_recv()

            @pl.when(s == 5)
            def _():
                self.fwd_ya.wait_recv()
                self.fwd_yb.wait_recv()

            @pl.when(s == 7)
            def _():
                self.fwd_da.wait_recv()
                self.fwd_db.wait_recv()

            at, copies = self.out_copies(s)
            self.consume(at)
            for c in copies:
                c.start()
            return carry

        lax.fori_loop(first, until, step, 0)

    def drain(self):
        for c in (self.own_p, self.own_xa, self.own_xb, self.own_ya, self.own_yb, self.relay_y, self.relay_x, self.fwd_xa,
                  self.fwd_xb, self.fwd_ya, self.fwd_yb, self.fwd_da, self.fwd_db):
            c.wait_send()

        def body(s, carry):
            for c in self.out_copies(s)[1]:
                c.wait()
            return carry

        lax.fori_loop(0, 8, body, 0)


class Refs:
    pass


def comm_call(body, ins, outs, scratch, cid, name, flops):
    in_names, out_names, scr_names = list(ins), list(outs), list(scratch)
    any_spec, vmem_spec = pl.BlockSpec(memory_space=pl.ANY), pl.BlockSpec(memory_space=pltpu.VMEM)
    arrays, in_specs = [], []
    for key in in_names:
        val = ins[key]
        in_specs.append(any_spec if isinstance(val, tuple) else vmem_spec)
        arrays.append(val[0] if isinstance(val, tuple) else val)

    def kernel(*refs):
        r = Refs()
        for key, ref in zip(in_names + out_names + scr_names, refs):
            setattr(r, key, ref)
        body(r)

    result = pl.pallas_call(
        kernel,
        in_specs=in_specs,
        out_specs=[any_spec if outs[key][2] else vmem_spec for key in out_names],
        out_shape=[jax.ShapeDtypeStruct(outs[key][0], outs[key][1]) for key in out_names],
        scratch_shapes=[scratch[key] for key in scr_names],
        compiler_params=pltpu.CompilerParams(collective_id=cid, has_side_effects=True, vmem_limit_bytes=VMEM_LIMIT),
        cost_estimate=pl.CostEstimate(flops=flops, bytes_accessed=30_000_000, transcendentals=0),
        name=name,
    )(*arrays)
    return dict(zip(out_names, result))


def fold8(vals):
    out = vals[0:8]
    for i in range(8, vals.shape[0], 8):
        out = out + vals[i:i + 8]
    return out


class Stage:
    def __init__(self, local, local_in, local_out=None, lhs=(), weight=(), weight_t=False, consume=None, cons_in=None,
                 cons_out=None, cons_acc=None, after=None):
        self.local, self.local_in, self.local_out = local, local_in, local_out or {}
        self.lhs, self.weight, self.weight_t = lhs, weight, weight_t
        self.consume, self.cons_in, self.cons_out, self.cons_acc = consume, cons_in or {}, cons_out or {}, cons_acc or {}
        self.after = after


def segment(cid, name, seq, width, stages, extra=None):
    rows = seq // 8
    half = rows // 2
    ins, outs, scratch = {}, {}, dict(extra or {})
    loads = []
    alias = [{} for _ in stages]

    def load(i, key, arr):
        tag = f"s{i}_{key}"
        ins[tag + "_h"] = (arr,)
        scratch[tag] = pltpu.VMEM(arr.shape, arr.dtype)
        loads.append(tag)
        alias[i][key] = tag

    flops = 100_000
    for i, st in enumerate(stages):
        for j, w in enumerate(st.weight):
            load(i, f"w{j}", w)
            if isinstance(st.lhs, str):
                alias[i]["lhs0"] = alias[i - 1][st.lhs]
            else:
                load(i, f"lhs{j}", st.lhs[j])
            flops += 2 * seq * width * LANES * 2
        for key, val in st.local_in.items():
            if isinstance(val, str):
                alias[i][key] = alias[i - 1][val]
            else:
                ins[f"s{i}_{key}"] = val
                alias[i][key] = f"s{i}_{key}"
        for key, (shape, dtype) in st.local_out.items():
            outs[f"s{i}_{key}"] = (shape, dtype, False)
            alias[i][key] = f"s{i}_{key}"
        if st.weight:
            scratch.update(rs_scratch(half, width))
        if st.consume:
            scratch.update(ag_scratch(seq, width))
            for key, arr in st.cons_in.items():
                load(i, key, arr)
            outs[f"s{i}_h_all"] = ((seq, width), BF16, True)
            for key, (cols, dtype) in st.cons_out.items():
                tag = f"s{i}_{key}"
                outs[tag + "_h"] = ((seq, cols), dtype, True)
                scratch[tag] = pltpu.VMEM((seq, cols), dtype)
                scratch[tag + "_s"] = pltpu.SemaphoreType.DMA((2, 8))
                alias[i][key] = tag
                flops += 2 * seq * width * cols
            for key, (shape, dtype) in st.cons_acc.items():
                outs[f"s{i}_{key}"] = (shape, dtype, False)
                alias[i][key] = f"s{i}_{key}"
    scratch["load_sem"] = pltpu.SemaphoreType.DMA((len(loads),))

    def body(r):
        pos = Place()
        pending = {}
        for n, tag in enumerate(loads):
            pending[tag] = pltpu.make_async_copy(getattr(r, tag + "_h"), getattr(r, tag), r.load_sem.at[n])
            pending[tag].start()

        def need(i, keys):
            for key in keys:
                copy = pending.pop(alias[i].get(key), None)
                if copy is not None:
                    copy.wait()

        barrier(pos)
        rs, ag, views = [], [], []
        for i, st in enumerate(stages):
            v = Refs()
            for key, tag in alias[i].items():
                setattr(v, key, getattr(r, tag))
            for key in scratch:
                if key.startswith(("h_", "sm_")):
                    setattr(v, key, getattr(r, key))
            views.append(v)
            pairs = [(f"lhs{j}", f"w{j}") for j in range(len(st.weight))]

            def produce(hf, block, cols, v=v, st=st, pairs=pairs):
                at = pl.ds(pl.multiple_of(block * rows + hf * half, half), half)
                total = None
                for a, w in pairs:
                    a, w = getattr(v, a), getattr(v, w)
                    part = dot_nt(a[at, :], w[cols, :]) if st.weight_t else dot_nn(a[at, :], w[:, cols])
                    total = part if total is None else total + part
                return total

            rs.append([ReduceScatter(pos, r, hf, half, width, functools.partial(produce, hf)) for hf in range(2)]
                      if st.weight else None)
            if st.consume:
                streams = [(r.h_vm, getattr(r, f"s{i}_h_all"), r.h_out)]
                for key in st.cons_out:
                    tag = alias[i][key]
                    streams.append((getattr(r, tag), getattr(r, tag + "_h"), getattr(r, tag + "_s")))
                ag.append([AllGather(pos, r, hf, half, functools.partial(st.consume, v), streams) for hf in range(2)])
            else:
                ag.append(None)

        def local(i, hf):
            reduced = None
            if rs[i]:
                rs[i][hf].finish()
                reduced = rs[i][hf].rows
            stages[i].local(views[i], pos, hf, half, reduced)
            if rs[i]:
                rs[i][hf].drain()
            if ag[i]:
                ag[i][hf].start()

        def front(i, hf):
            need(i, [f"{kind}{j}" for j in range(len(stages[i].weight)) for kind in ("lhs", "w")])
            rs[i][hf].compute(send=hf == 0)

        for i, st in enumerate(stages):
            before = ag[i - 1] if i else None
            if rs[i]:
                if before:
                    before[0].drain()
                front(i, 0)
            if before:
                before[1].use(0, 2)
                before[1].second()
                before[1].use(2, 6)
                before[1].last()
                before[1].use(6, 8)
                before[1].drain()
            if rs[i]:
                front(i, 1)
                rs[i][0].relay()
                rs[i][1].send_all()
            if ag[i]:
                need(i, list(st.cons_in))
                for key in st.cons_acc:
                    ref = getattr(views[i], key)
                    ref[...] = jnp.zeros_like(ref)
            local(i, 0)
            if rs[i]:
                if ag[i]:
                    ag[i][0].use(0, 2)
                rs[i][1].relay()
            local(i, 1)
            if ag[i]:
                ag[i][0].relay()
                if not rs[i]:
                    ag[i][0].use(0, 2)
                ag[i][0].second()
                ag[i][0].use(2, 6)
                ag[i][1].relay()
                ag[i][0].last()
                ag[i][0].use(6, 8)
        if ag[-1]:
            ag[-1][1].use(0, 2)
            ag[-1][1].second()
            ag[-1][1].use(2, 6)
            ag[-1][1].last()
            ag[-1][1].use(6, 8)
            for one in ag[-1]:
                one.drain()
        if stages[-1].after:
            stages[-1].after(views[-1], pos)

    res = comm_call(body, ins, outs, scratch, cid, name, flops)
    made = []
    for i in range(len(stages)):
        tag = f"s{i}_"
        made.append({key[len(tag):].removesuffix("_h"): val for key, val in res.items() if key.startswith(tag)})
    return made


STEP_ROWS = 16


def normalize(res):
    mean = jnp.mean(res, axis=-1, keepdims=True)
    centered = res - mean
    var = jnp.mean(centered * centered, axis=-1, keepdims=True)
    rstd = lax.rsqrt(var + 1e-5)
    return centered * rstd, rstd


def local_forward(with_sum, with_h):
    def run(v, pos, hf, half, reduced):
        def step(i, carry):
            inner = pl.multiple_of(i * STEP_ROWS, STEP_ROWS)
            at = pl.multiple_of(hf * half + inner, STEP_ROWS)
            here = pl.ds(at, STEP_ROWS)
            res = v.res[here, :].astype(F32)
            if with_sum:
                res = (res + reduced(inner, STEP_ROWS)) + v.ln[2:, :]
                v.res_out[here, :] = res.astype(v.res_out.dtype)
            if with_h:
                xhat, _ = normalize(res)
                v.h_vm[pl.ds(pl.multiple_of(pos.me * 2 * half + at, STEP_ROWS), STEP_ROWS), :] = (
                    xhat * v.ln[0:1, :] + v.ln[1:2, :]).astype(BF16)
            return carry

        lax.fori_loop(0, half // STEP_ROWS, step, 0)

    return run


def local_backward(last):
    def run(v, pos, hf, half, reduced):
        def step(i, carry):
            d_gain, d_shift, d_bias = carry
            inner = pl.multiple_of(i * STEP_ROWS, STEP_ROWS)
            at = pl.multiple_of(hf * half + inner, STEP_ROWS)
            here = pl.ds(at, STEP_ROWS)
            d_h = reduced(inner, STEP_ROWS)
            xhat, rstd = normalize(v.res[here, :].astype(F32))
            d_gain = d_gain + fold8(d_h * xhat)
            d_shift = d_shift + fold8(d_h)
            d_hat = d_h * v.ln[0:1, :]
            m_one = jnp.mean(d_hat, axis=-1, keepdims=True)
            m_two = jnp.mean(d_hat * xhat, axis=-1, keepdims=True)
            d_out = v.d_res[here, :].astype(F32) + rstd * (d_hat - m_one - xhat * m_two)
            d_bias = d_bias + fold8(d_out)
            v.d_out[here, :] = d_out.astype(v.d_out.dtype)
            if not last:
                v.h_vm[pl.ds(pl.multiple_of(pos.me * 2 * half + at, STEP_ROWS), STEP_ROWS), :] = d_out.astype(BF16)
            return d_gain, d_shift, d_bias

        zero = jnp.zeros((8, v.ln.shape[-1]), F32)
        totals = lax.fori_loop(0, half // STEP_ROWS, step, (zero, zero, zero))
        for n, total in enumerate(totals):
            row = slice(n, n + 1)
            total = jnp.sum(total, axis=0, keepdims=True)
            v.sums[row, :] = v.sums[row, :] + total if hf else total

    return run


def small_scratch(width):
    shape = (3, 16, width)
    return dict(sm_snd=pltpu.VMEM(shape, F32), sm_rcv=pltpu.VMEM(shape, F32), sm_send=pltpu.SemaphoreType.DMA((3,)),
                sm_recv=pltpu.SemaphoreType.DMA((3,)))


def small_sum(v, pos):
    v.sm_snd[0] = v.small[...]
    v.sm_snd[0, 0:2, :] = v.sums[0:2, :]
    sems = (v.sm_send, v.sm_recv)
    copies = []
    for i, peer in enumerate((pos.partner, pos.xn, pos.yn)):
        c = rdma(v.sm_snd.at[i], v.sm_rcv.at[i], sems, i, peer)
        c.start()
        c.wait_recv()
        copies.append(c)
        total = v.sm_snd[i] + v.sm_rcv[i]
        if i < 2:
            v.sm_snd[i + 1] = total
        else:
            v.small_out[...] = total
    for c in copies:
        c.wait_send()


GELU_C = math.sqrt(2.0 / math.pi)


def gelu_pair(x):
    sq = x * x
    t = jnp.tanh(GELU_C * x * (1.0 + 0.044715 * sq))
    half = 0.5 * (1.0 + t)
    grad = half + (0.5 * GELU_C) * x * (1.0 - t * t) * (1.0 + (3 * 0.044715) * sq)
    return x * half, grad


def consume_qkv(r, at):
    h = r.h_vm[at, :]
    for c in range(0, r.qkv.shape[1], 256):
        cols = pl.ds(c, 256)
        r.qkv[at, cols] = dot_nt(h, r.wqkv[cols, :]).astype(BF16)


def consume_up(r, at):
    h = r.h_vm[at, :]
    for c in range(0, r.act.shape[1], 256):
        cols = pl.ds(c, 256)
        act, grad = gelu_pair(dot_nn(h, r.w_up[:, cols]) + r.b_up[:, cols])
        r.act[at, cols] = act.astype(BF16)
        r.gel[at, cols] = grad


def consume_up_down(r, at):
    h = r.h_vm[at, :]
    dy = r.dy[at, :]
    for c in range(0, r.act.shape[1], 256):
        cols = pl.ds(c, 256)
        act, grad = gelu_pair(dot_nn(h, r.w_up[:, cols]) + r.b_up[:, cols])
        r.act[at, cols] = act.astype(BF16)
        d_pre = dot_nt(dy, r.w_down[cols, :]) * grad
        r.d_bup[:, cols] += fold8(d_pre)
        r.d_pre[at, cols] = d_pre.astype(BF16)


def consume_dpre(r, at):
    d = r.h_vm[at, :]
    for c in range(0, r.d_pre.shape[1], 256):
        cols = pl.ds(c, 256)
        d_pre = dot_nt(d, r.w_down[cols, :]) * r.gel[at, cols]
        r.d_bup[:, cols] += fold8(d_pre)
        r.d_pre[at, cols] = d_pre.astype(BF16)


def consume_dattn(r, at):
    r.d_attn[at, :] = dot_nt(r.h_vm[at, :], r.w_out[...]).astype(BF16)


def spec(text):
    return P(*[dict(d="dp", t="tp").get(letter) for letter in text])


def stack_all(groups):
    return [jnp.stack(group) for group in groups]


def solution(mesh):
    def device_step(x_loc, dy_loc, ln_par, bias_d, w_qkv, w_out, w_up, b_up, w_down):
        (x_in,), (dy,) = x_loc, dy_loc
        rows, width = x_in.shape
        seq = rows * mesh.shape['tp']
        n_heads, head_dim = w_qkv.shape[-2:]
        ff = w_up.shape[-1]
        lanes = n_heads * LANES

        def pad_heads(w):
            flat = w.reshape((-1, head_dim, width))
            return jnp.concatenate([flat, jnp.zeros((flat.shape[0], LANES - head_dim, width), BF16)], axis=1).reshape((-1, width))

        wqkv_t = [pad_heads(jnp.moveaxis(w, 0, -1)) for w in w_qkv]
        wo = [pad_heads(w) for w in w_out]
        parts = [w.reshape((-1, lanes, width)) for w in wqkv_t]
        (up_a, up_b), (down_a, down_b), (wq_a, wq_b), (wo_a, wo_b) = w_up, w_down, wqkv_t, wo
        bup_a, bup_b = jnp.split(b_up, 2)
        (gain_a, shift_a, gain_b, shift_b), (gain_c, shift_c, gain_d, shift_d) = ln_par
        (bias_a, bias_b), (bias_c, bias_d2) = bias_d
        part_a, part_b = [list(w) for w in parts]

        f32_rows = ((rows, width), F32)
        bf_rows = ((rows, width), BF16)
        sums = ((8, width), F32)
        keep = dict(res_out=f32_rows)
        back = dict(d_out=f32_rows, sums=sums)
        qkv_out = dict(qkv=(len(wq_a), BF16))
        dattn_out = dict(d_attn=(lanes, BF16))
        bup_acc = dict(d_bup=((8, ff), F32))
        enter, middle, leave = local_forward(False, True), local_forward(True, True), local_forward(True, False)
        backward = local_backward(False)
        act_out = dict(act=(ff, BF16))

        (u0,) = segment(0, "ag_qkv", seq, width, [Stage(
            enter, dict(res=x_in, ln=jnp.stack([gain_a, shift_a])), consume=consume_qkv, cons_in=dict(wqkv=wq_a), cons_out=qkv_out)])
        qkv_a = u0["qkv"]
        dy_dep, _ = lax.optimization_barrier((dy, qkv_a))
        dy_all = lax.all_gather(dy_dep, 'tp', axis=0, tiled=True)

        attn_a, lse_a = attention_forward(qkv_a, head_dim, n_heads)
        u1, u2 = segment(1, "mid_fwd", seq, width, [
            Stage(middle, dict(res=x_in, ln=jnp.stack([gain_b, shift_b, bias_a])), keep, lhs=[attn_a], weight=[wo_a],
                  consume=consume_up, cons_in=dict(w_up=up_a, b_up=bup_a), cons_out=dict(act_out, gel=(ff, F32))),
            Stage(middle, dict(res="res_out", ln=jnp.stack([gain_c, shift_c, bias_b])), keep, lhs="act", weight=[down_a],
                  consume=consume_qkv, cons_in=dict(wqkv=wq_b), cons_out=qkv_out)])
        qkv_b = u2["qkv"]
        attn_b, lse_b = attention_forward(qkv_b, head_dim, n_heads)
        u3, u5 = segment(2, "turn", seq, width, [
            Stage(middle, dict(res=u2["res_out"], ln=jnp.stack([gain_d, shift_d, bias_c])), keep, lhs=[attn_b], weight=[wo_b],
                  consume=consume_up_down, cons_in=dict(w_up=up_b, b_up=bup_b, dy=dy_all, w_down=down_b),
                  cons_out=dict(act_out, d_pre=(ff, BF16)), cons_acc=bup_acc),
            Stage(backward, dict(res="res_out", d_res=dy, ln=gain_d[None]), back, lhs="d_pre", weight=[up_b], weight_t=True,
                  consume=consume_dattn, cons_in=dict(w_out=wo_b), cons_out=dattn_out)])
        (u4,) = segment(3, "down_y", seq, width, [Stage(
            leave, dict(res=u3["res_out"], ln=jnp.stack([gain_d, shift_d, bias_d2])), dict(res_out=bf_rows), lhs=[u3["act"]],
            weight=[down_b])])
        dqkv_b = attention_backward(qkv_b, attn_b, u5["d_attn"], lse_b, head_dim, n_heads)
        u6, u7 = segment(4, "mid_bwd", seq, width, [
            Stage(backward, dict(res=u2["res_out"], d_res=u5["d_out"], ln=gain_c[None]), back, lhs=list(dqkv_b), weight=part_b,
                  consume=consume_dpre, cons_in=dict(w_down=down_a, gel=u1["gel"]), cons_out=dict(d_pre=(ff, BF16)),
                  cons_acc=bup_acc),
            Stage(backward, dict(res=u1["res_out"], d_res="d_out", ln=gain_b[None]), back, lhs="d_pre", weight=[up_a],
                  weight_t=True, consume=consume_dattn, cons_in=dict(w_out=wo_a), cons_out=dattn_out)])
        dqkv_a = attention_backward(qkv_a, attn_a, u7["d_attn"], lse_a, head_dim, n_heads)
        u7_sums, u6_sums, u5_sums = [u["sums"][:3] for u in (u7, u6, u5)]
        pair = jnp.zeros((2, width), F32)
        small = jnp.concatenate([pair, u7_sums, u6_sums, u5_sums, jnp.sum(dy.astype(F32), axis=0, keepdims=True), pair, pair])
        (u8,) = segment(5, "end_bwd", seq, width, [Stage(
            local_backward(True), dict(res=x_in, d_res=u7["d_out"], ln=gain_a[None], small=small),
            dict(d_out=bf_rows, sums=sums, small_out=((16, width), F32)), lhs=list(dqkv_a), weight=part_a, after=small_sum)],
            small_scratch(width))
        g0, s0, g1, s1, b0, g2, s2, b1, g3, s3, b2, b3 = u8["small_out"][:12]
        ln_grad = jnp.stack(stack_all([[g0, s0, g1, s1], [g2, s2, g3, s3]]))
        bias_grad = jnp.stack(stack_all([[b0, b1], [b2, b3]]))

        def grads(lefts, rights):
            return [dot_tn(a, b).astype(BF16) for a, b in zip(lefts, rights)]

        def drop_pad(g):
            return g.reshape((-1, LANES, width))[:, :head_dim]

        g_down = grads([u1["act"], u3["act"]], [u6["h_all"], dy_all])
        g_up = grads([u1["h_all"], u3["h_all"]], [u6["d_pre"], u3["d_pre"]])
        g_out = [drop_pad(g) for g in grads([attn_a, attn_b], [u7["h_all"], u5["h_all"]])]
        g_qkv = [jnp.stack([drop_pad(g) for g in grads(d, [h] * len(d))])
                 for d, h in ((dqkv_a, u0["h_all"]), (dqkv_b, u2["h_all"]))]
        d_bup = [jnp.sum(u["d_bup"], axis=0) for u in (u6, u3)]
        g_qkv, g_out, g_up, d_bup, g_down = stack_all([g_qkv, g_out, g_up, d_bup, g_down])
        return (u4["res_out"][None], u8["d_out"][None], ln_grad, bias_grad, jnp.moveaxis(g_qkv, -1, 1), g_out, g_up, d_bup, g_down)

    tokens, rep = spec("dtn"), spec("nnn")
    in_specs = (tokens, tokens, rep, rep, spec("nnntn"), spec("ntnn"), spec("nnt"), spec("nt"), spec("ntn"))
    out_specs = (tokens, tokens, spec("dnn"), spec("dnn"), spec("dnntn"), spec("dtnn"), spec("dnt"), spec("dt"), spec("dtn"))
    return jax.shard_map(device_step, mesh=mesh, in_specs=in_specs, out_specs=out_specs, check_vma=False)
```

time: 780 us -> 775 us (level)
    pallas_call x9 -> x6, Pallas kernels: 560 us -> 557 us  [comm_call(): pl.pallas_call(kernel, in_specs=in_specs, out_specs=[any_spec if outs[key...]
where the time goes in v2:
time: 775 us; the launch traced here: 765 us
  Pallas kernels  627 us (81%)
  matrix products  64.2 us (8%)
  local copies, waits for them, and re-layouts  45.7 us (6%)
  between operations  15.2 us (2%)
  other arithmetic  13 us (2%)
    pallas_call x6, Pallas kernels, comm_call(): pl.pallas_call(kernel, in_specs=in_specs, out_specs=[any_spec if outs[key...  557 us
    dot_general x12, matrix products, dot_tn(): lax.dot_general(a, b, (((0,), (0,)), ((), ())), preferred_element_type=F32)  64.2 us
    pallas_call x2, Pallas kernels, attention_backward(): pl.pallas_call(functools.partial(attn_bwd_kernel, head_dim ** (-0.5), n_q...  37.3 us
    pallas_call x2, Pallas kernels, attention_forward(): pl.pallas_call(functools.partial(attn_fwd_kernel, head_dim ** (-0.5), n_q...  33.1 us
  transfers between devices with their start and end apart: 1, of which 0 were waited for; matrix products, arithmetic and copies ran while one was open for 2% of the time, Pallas kernels for 23%

profile of v2, /device:TPU:0, one launch (start us, length us, event | category | flops | bytes accessed | tf_op | source)
XLA Modules:
  0.0 765.1 jit_solution(7196912959122082033)
XLA Ops:
  7.2 1.0 slice_bitcast_fusion.19
  8.3 3.6 fusion.4
  12.5 1.6 concatenate.20
  14.1 42.0 %ag_qkv.1 = (bf16[2048,1536]{1,0:T(8,128)(2,1)}, bf16[2048,768]{1,0:T(8,128)(2,1)}) custom-call(bf16[256,1536]{1,0:T(8,128)(2,1)} %bitcast.169, f32[2,1536]{1,0:T(2,128)} %pad_maximum_fusion.10.refs_1_, bf16[768,1536]{1,0:T(8,128)(2,1)} %bitcast.155), custom_call_target="tpu_custom_call" | custom-call | flops 4831938048 | bytes 30000000 | tf_op jit(solution)/shard_map/ag_qkv/pallas_call | solution.py:408
  56.3 1.4 slice_bitcast_fusion.12
  57.8 0.9 concatenate.19
  58.7 0.9 concatenate.18
  59.6 1.7 concatenate.21
  61.3 16.4 %attn_fwd.2 = (bf16[2048,256]{1,0:T(8,128)(2,1)S(1)}, f32[2,1,2048]{2,1,0:T(1,128)S(1)}) custom-call(bf16[2048,768]{1,0:T(8,128)(2,1)S(1)} %copy-done, bf16[2048,768]{1,0:T(8,128)(2,1)S(1)} %copy-done, bf16[2048,768]{1,0:T(8,128)(2,1)S(1)} %copy-done), custom_call_target="tpu_custom_call" | custom-call | flops 2147483648 | bytes 4194304 | tf_op jit(solution)/shard_map/attn_fwd/pallas_call | solution.py:71
  79.1 2.5 slice_bitcast_fusion
  82.0 2.5 slice_bitcast_fusion.1
  84.5 140.0 %mid_fwd.1 = (f32[256,1536]{1,0:T(8,128)}, bf16[2048,1536]{1,0:T(8,128)(2,1)}, bf16[2048,768]{1,0:T(8,128)(2,1)}, f32[2048,768]{1,0:T(8,128)}, f32[256,1536]{1,0...) custom-call(bf16[256,1536]{1,0:T(8,128)(2,1)} %bitcast.156, bf16[2048,256]{1,0:T(8,128)(2,1)} %copy-done.3, ...), custom_call_target="tpu_custom_call" | custom-call | flops 17716840448 | bytes 30000000 | tf_op jit(solution)/shard_map/mid_fwd/pallas_call | solution.py:408
  224.5 1.9 copy-done.1
  226.4 16.8 %attn_fwd.3 = (bf16[2048,256]{1,0:T(8,128)(2,1)S(1)}, f32[2,1,2048]{2,1,0:T(1,128)S(1)}) custom-call(bf16[2048,768]{1,0:T(8,128)(2,1)S(1)} %copy-done.1, bf16[2048,768]{1,0:T(8,128)(2,1)S(1)} %copy-done.1, bf16[2048,768]{1,0:T(8,128)(2,1)S(1)} %copy-done.1), custom_call_target="tpu_custom_call" | custom-call | flops 2147483648 | bytes 4194304 | tf_op jit(solution)/shard_map/attn_fwd/pallas_call | solution.py:71
  243.2 1.0 copy-done.6
  244.8 1.6 pad_slice_fusion.3
  246.4 1.5 pad_slice_fusion
  247.9 144.3 %turn.1 = (f32[256,1536]{1,0:T(8,128)}, bf16[2048,1536]{1,0:T(8,128)(2,1)}, bf16[2048,768]{1,0:T(8,128)(2,1)}, bf16[2048,768]{1,0:T(8,128)(2,1)}, f32[8,768]{1,0...) custom-call(bf16[256,1536]{1,0:T(8,128)(2,1)} %bitcast.159, ...), custom_call_target="tpu_custom_call" | custom-call | flops 14495614976 | bytes 30000000 | tf_op jit(solution)/shard_map/turn/pallas_call | solution.py:408
  393.0 1.9 copy-done.2
  394.9 1.2 copy-done.7
  396.1 1.2 copy-done.16
  397.4 18.6 %attn_bwd.2 = (bf16[2048,256]{1,0:T(8,128)(2,1)S(1)}, bf16[2048,256]{1,0:T(8,128)(2,1)S(1)}, bf16[2048,256]{1,0:T(8,128)(2,1)S(1)}) custom-call(bf16[2048,768]{1,0:T(8,128)(2,1)S(1)} %copy-done.2, bf16[2048,768]{1,0:T(8,128)(2,1)S(1)} %copy-done.2, bf16[2048,768]{1,0:T(8,128)(2,1)S(1)} %copy-done.2, bf16[2048,256]{1,0:T(8,128)(2,1)S(1)} %copy-done.7, ...), custom_call_target="tpu_custom_call" | custom-call | flops 5368709120 | bytes 8388608 | tf_op jit(solution)/shard_map/attn_bwd/pallas_call | solution.py:134
  416.0 6.6 convolution_convert_fusion.8
  422.6 5.6 convolution_convert_fusion.6
  428.2 2.7 convolution_convert_fusion.7
  431.0 145.9 %mid_bwd.1 = (f32[256,1536]{1,0:T(8,128)}, f32[8,1536]{1,0:T(8,128)}, bf16[2048,1536]{1,0:T(8,128)(2,1)}, bf16[2048,768]{1,0:T(8,128)(2,1)}, f32[8,768]{1,0:T(8,...) custom-call(bf16[256,1536]{1,0:T(8,128)(2,1)} %bitcast.165, ...), custom_call_target="tpu_custom_call" | custom-call | flops 12885002240 | bytes 30000000 | tf_op jit(solution)/shard_map/mid_bwd/pallas_call | solution.py:408
  578.5 1.2 copy-done.4
  579.7 1.2 copy-done.15
  580.9 18.7 %attn_bwd.3 = (bf16[2048,256]{1,0:T(8,128)(2,1)S(1)}, bf16[2048,256]{1,0:T(8,128)(2,1)S(1)}, bf16[2048,256]{1,0:T(8,128)(2,1)S(1)}) custom-call(bf16[2048,768]{1,0:T(8,128)(2,1)S(1)} %copy-done, bf16[2048,768]{1,0:T(8,128)(2,1)S(1)} %copy-done, bf16[2048,768]{1,0:T(8,128)(2,1)S(1)} %copy-done, bf16[2048,256]{1,0:T(8,128)(2,1)S(1)} %copy-done.4, ...), custom_call_target="tpu_custom_call" | custom-call | flops 5368709120 | bytes 8388608 | tf_op jit(solution)/shard_map/attn_bwd/pallas_call | solution.py:134
  599.7 6.6 convolution_convert_fusion.9
  606.3 5.7 convolution_convert_fusion.10
  612.0 2.7 convolution_convert_fusion.11
  614.7 1.3 concatenate.23.refs_9_
  616.0 48.0 %end_bwd.1 = (bf16[256,1536]{1,0:T(8,128)(2,1)}, f32[8,1536]{1,0:T(8,128)}, f32[16,1536]{1,0:T(8,128)}) custom-call(bf16[256,1536]{1,0:T(8,128)(2,1)} %bitcast.162, bf16[2048,256]{1,0:T(8,128)(2,1)} %copy-done.12, bf16[256,1536]{1,0:T(8,128)(2,1)} %bitcast.163, bf16[2048,256]{1,0:T(8,128)(2,1)} %copy-done.13, bf16[256,1536]{1,0:T(8,128)(2,1)} %bitcast.161, ...), custom_call_target="tpu_custom_call" | custom-call | flops 4831938048 | bytes 30000000 | tf_op jit(solution)/shard_map/end_bwd/pallas_call | solution.py:408
  666.6 4.6 convolution_convert_fusion.4
  671.3 36.3 %down_y.1 = bf16[256,1536]{1,0:T(8,128)(2,1)} custom-call(bf16[768,1536]{1,0:T(8,128)(2,1)} %get-tuple-element.90.refs_7_.refs_0_, bf16[2048,768]{1,0:T(8,128)(2,1)} %get-tuple-element.54.refs_1_, f32[256,1536]{1,0:T(8,128)} %get-tuple-element.55.refs_2_, f32[3,1536]{1,0:T(4,128)} %get-tuple-element.118.refs_3_), custom_call_target="tpu_custom_call" | custom-call | flops 1610712704 | bytes 30000000 | tf_op jit(solution)/shard_map/down_y/pallas_call | solution.py:408
  707.6 0.9 slice_bitcast_fusion.4
  709.4 1.9 slice_bitcast_fusion.7
  712.1 4.7 convolution_convert_fusion.5
  718.2 1.4 copy-done.45
  719.7 8.3 %fusion.2 = bf16[1,768,1536]{2,1,0:T(8,128)(2,1)S(1)} fusion(bf16[2048,768]{1,0:T(8,128)(2,1)S(1)} %copy-done.45, bf16[2048,1536]{1,0:T(8,128)(2,1)} %get-tuple-element.86), kind=kOutput, calls=%fused_computation.9 | convolution fusion | flops 4833017856 | bytes 11796480 | tf_op jit(solution)/shard_map/dot_general | solution.py:28
  728.0 5.4 fusion.3
  733.5 2.8 pad_maximum_fusion.1
  736.6 5.7 fusion
  742.4 1.1 pad_maximum_fusion.2
  744.5 2.1 maximum_bitcast_fusion
  747.9 5.5 fusion.1
  753.5 2.6 pad_maximum_fusion
  (156 shorter events, 15.9 us)
Async XLA Ops:
  7.2 240.7 %all-gather.2.cloned.1.call-start = ((), (), s32[]{:S(2)}) async-start(), calls=%async_computation | async-start | bytes 7077888 | tf_op jit(solution)/shard_map/all_gather | solution.py:790
  8.2 3.6 copy-start.39
  8.2 70.2 %copy-start.40 = (f32[1,1536]{1,0:T(1,128)}, f32[1,1536]{1,0:T(1,128)S(1)}, u32[]{:S(2)}) copy-start(f32[1,1536]{1,0:T(1,128)S(1)} %get-tuple-element.108.refs_8_) | copy-start | bytes 18436
  8.2 70.2 %copy-start.41 = (f32[1,1536]{1,0:T(1,128)}, f32[1,1536]{1,0:T(1,128)S(1)}, u32[]{:S(2)}) copy-start(f32[1,1536]{1,0:T(1,128)S(1)} %get-tuple-element.110.refs_13_) | copy-start | bytes 18436
  8.2 235.9 %copy-start.35 = (f32[1,1536]{1,0:T(1,128)}, f32[1,1536]{1,0:T(1,128)S(1)}, u32[]{:S(2)}) copy-start(f32[1,1536]{1,0:T(1,128)S(1)} %get-tuple-element.106.refs_10_) | copy-start | bytes 18436
  11.8 44.3 %copy-start.19 = (bf16[1,1536,3,2,96]{1,4,3,2,0:T(8,128)(2,1)}, bf16[1,1536,3,2,96]{1,4,3,2,0:T(8,128)(2,1)S(1)}, u32[]{:S(2)}) copy-start(bf16[1,1536,3,2,96]{1,4,3,2,0:T(8,128)(2,1)S(1)} %get-tuple-element.92) | copy-start | bytes 5308420
  14.1 42.1 %copy-start.23 = (bf16[1,256,1536]{2,1,0:T(8,128)(2,1)S(1)}, bf16[1,256,1536]{2,1,0:T(8,128)(2,1)}, u32[]{:S(2)}) copy-start(bf16[1,256,1536]{2,1,0:T(8,128)(2,1)} %param.10) | copy-start | bytes 2359300
  56.2 3.5 copy-start.17
  57.8 3.6 copy-start
  59.6 19.4 %slice-start.4 = ((s8[4718592]{0:T(1024)(128)(4,1)}), s8[4194304]{0:T(1024)(128)(4,1)S(1)}, s32[]{:S(2)}) async-start(s8[4718592]{0:T(1024)(128)(4,1)} %bitcast.139), calls=%async_computation.5 | async-start | bytes 8388608
  61.3 16.4 %copy-start.42 = (f32[2,768]{1,0:T(2,128)S(1)}, f32[2,768]{1,0:T(2,128)}, u32[]{:S(2)}) copy-start(f32[2,768]{1,0:T(2,128)} %param.16) | copy-start | bytes 18436
  61.3 17.0 %copy-start.36 = (f32[2,2,1536]{2,1,0:T(2,128)S(1)}, f32[2,2,1536]{2,1,0:T(2,128)}, u32[]{:S(2)}) copy-start(f32[2,2,1536]{2,1,0:T(2,128)} %param.12) | copy-start | bytes 73732
  61.3 17.8 %slice-start.5 = ((s8[4718592]{0:T(1024)(128)(4,1)}), s8[524288]{0:T(1024)(128)(4,1)S(1)}, s32[]{:S(2)}) async-start(s8[4718592]{0:T(1024)(128)(4,1)} %bitcast.139), calls=%async_computation.6 | async-start | bytes 1048576
  77.7 3.9 copy-start.3
  78.4 3.1 slice-start.6
  226.4 18.4 %copy-start.20 = (bf16[1,1536,3,2,96]{1,4,3,2,0:T(8,128)(2,1)S(1)}, bf16[1,1536,3,2,96]{1,4,3,2,0:T(8,128)(2,1)}, u32[]{:S(2)}) copy-start(bf16[1,1536,3,2,96]{1,4,3,2,0:T(8,128)(2,1)} %copy-done.19) | copy-start | bytes 5308420
  415.9 6.7 copy-start.9
  415.9 6.7 copy-start.11
  416.0 12.3 %copy-start.10 = (bf16[2048,256]{1,0:T(8,128)(2,1)}, bf16[2048,256]{1,0:T(8,128)(2,1)S(1)}, u32[]{:S(2)}) copy-start(bf16[2048,256]{1,0:T(8,128)(2,1)S(1)} %get-tuple-element.59.refs_3_) | copy-start | bytes 3145732
  416.0 12.3 %slice-start.2 = ((s8[6291456]{0:T(1024)(128)(4,1)}), s8[4194304]{0:T(1024)(128)(4,1)S(1)}, s32[]{:S(2)}) async-start(s8[6291456]{0:T(1024)(128)(4,1)} %bitcast.133), calls=%async_computation.3 | async-start | bytes 8388608
  422.6 5.6 slice-start.3
  599.7 6.7 copy-start.14
  599.7 6.7 copy-start.13
  599.7 12.3 %copy-start.12 = (bf16[2048,256]{1,0:T(8,128)(2,1)}, bf16[2048,256]{1,0:T(8,128)(2,1)S(1)}, u32[]{:S(2)}) copy-start(bf16[2048,256]{1,0:T(8,128)(2,1)S(1)} %get-tuple-element.66.refs_1_) | copy-start | bytes 3145732
  599.7 12.3 %slice-start = ((s8[6291456]{0:T(1024)(128)(4,1)}), s8[4194304]{0:T(1024)(128)(4,1)S(1)}, s32[]{:S(2)}) async-start(s8[6291456]{0:T(1024)(128)(4,1)} %bitcast.131), calls=%async_computation.1 | async-start | bytes 8388608
  606.3 5.7 slice-start.1
  616.0 50.6 %copy-start.8 = (bf16[2048,256]{1,0:T(8,128)(2,1)S(1)}, bf16[2048,256]{1,0:T(8,128)(2,1)}, u32[]{:S(2)}) copy-start(bf16[2048,256]{1,0:T(8,128)(2,1)} %copy-done.6) | copy-start | bytes 3145732
  671.2 37.2 %copy-start.37 = (f32[8,768]{1,0:T(8,128)S(1)}, f32[8,768]{1,0:T(8,128)}, u32[]{:S(2)}) copy-start(f32[8,768]{1,0:T(8,128)} %get-tuple-element.84) | copy-start | bytes 73732
  671.2 37.3 %copy-start.25 = (bf16[256,1536]{1,0:T(8,128)(2,1)S(1)}, bf16[256,1536]{1,0:T(8,128)(2,1)}, u32[]{:S(2)}) copy-start(bf16[256,1536]{1,0:T(8,128)(2,1)} %convolution_convert_fusion.8) | copy-start | bytes 2359300
  707.5 3.7 copy-start.24
  707.5 4.6 copy-start.5
  712.1 5.6 copy-start.38
  712.1 5.6 copy-start.28
  712.1 5.7 copy-start.27
  717.8 10.2 %slice-start.8 = ((s8[6291456]{0:T(1024)(128)(4,1)}), s8[4194304]{0:T(1024)(128)(4,1)S(1)}, s32[]{:S(2)}) async-start(s8[6291456]{0:T(1024)(128)(4,1)} %bitcast.167), calls=%async_computation.9 | async-start | bytes 8388608
  719.7 8.3 %copy-start.22 = (bf16[2048,768]{1,0:T(8,128)(2,1)S(1)}, bf16[2048,768]{1,0:T(8,128)(2,1)}, u32[]{:S(2)}) copy-start(bf16[2048,768]{1,0:T(8,128)(2,1)} %get-tuple-element.54.refs_1_) | copy-start | bytes 9437188
  719.7 8.3 %slice-start.9 = ((s8[6291456]{0:T(1024)(128)(4,1)}), s8[2097152]{0:T(1024)(128)(4,1)S(1)}, s32[]{:S(2)}) async-start(s8[6291456]{0:T(1024)(128)(4,1)} %bitcast.167), calls=%async_computation.10 | async-start | bytes 4194304
  719.7 16.6 %slice-start.10 = ((s8[6291456]{0:T(1024)(128)(4,1)}), s8[4194304]{0:T(1024)(128)(4,1)S(1)}, s32[]{:S(2)}) async-start(s8[6291456]{0:T(1024)(128)(4,1)} %bitcast.172), calls=%async_computation.11 | async-start | bytes 8388608
  728.0 8.3 %slice-start.11 = ((s8[6291456]{0:T(1024)(128)(4,1)}), s8[2097152]{0:T(1024)(128)(4,1)S(1)}, s32[]{:S(2)}) async-start(s8[6291456]{0:T(1024)(128)(4,1)} %bitcast.172), calls=%async_computation.12 | async-start | bytes 4194304
  733.5 14.5 %slice-start.12 = ((s8[6291456]{0:T(1024)(128)(4,1)}), s8[4194304]{0:T(1024)(128)(4,1)S(1)}, s32[]{:S(2)}) async-start(s8[6291456]{0:T(1024)(128)(4,1)} %bitcast.174), calls=%async_computation.13 | async-start | bytes 8388608
  736.6 5.8 copy-start.32
  736.6 5.8 copy-start.33
  736.6 7.5 copy-start.29
  736.6 7.5 copy-start.30
  736.6 7.5 copy-start.31
  736.6 11.3 %slice-start.13 = ((s8[6291456]{0:T(1024)(128)(4,1)}), s8[2097152]{0:T(1024)(128)(4,1)S(1)}, s32[]{:S(2)}) async-start(s8[6291456]{0:T(1024)(128)(4,1)} %bitcast.174), calls=%async_computation.14 | async-start | bytes 4194304
  744.5 3.4 copy-start.43
  753.4 3.5 copy-start.34
  (13 other events, 23.8 us)
Sparse Core Ops, SparseCore 0:
  56.3 42.5 all-gather.1
